TPU v7x, 128 devices: a whole 4x4x4 slice. The times are simulated.
128 devices in a mesh: row: 32 (over y, x, core), col: 4 (over z).
Axes of the slice: x: 4, y: 4, z: 4, core: 2. Of those that a mesh axis runs over, the one named last changes fastest.
Arguments:
- stiff_bb: bfloat16 [384, 3, 128, 384], P(('row', 'col')), may hold values from -6 to 6
- stiff_bi: bfloat16 [384, 384, 3072], P(('row', 'col')), may hold values from -6 to 6
- constraint_modes: bfloat16 [384, 3072, 384], P(('row', 'col')), may hold values from -0.109375 to 0.109375
- interior_mass: float32 [384, 3072], P(('row', 'col')), may hold values from 0.25 to 4
- fixed_modes: bfloat16 [384, 3072, 256], P(('row', 'col')), may hold values from -6 to 6
- mass_bb: bfloat16 [384, 3, 128, 384], P(('row', 'col')), may hold values from -6 to 6
- boundary_map: int32 [384, 3], P(('row', 'col')), may hold values from 0 to 767, as said below
Outputs:
- interface_stiffness: float32 [768, 4, 128, 128], P('row', None, 'col')
- interface_mass: float32 [768, 4, 128, 128], P('row', None, 'col')
- mass_coupling: float32 [384, 256, 384], P(('row', 'col'))
Inputs may be any that keep to these rules, and one draw needn't show every extreme that they name: `boundary_map`: row s holds blocks b, b + a, b + c with 0 < a < c < 4, all three in the range of one owner (block // 24). Rows come in aligned row groups of 12; no owner serves more than 1 row of one row group, and in every draw one owner serves exactly 1 row of every row group.
All inputs are finite; a program needn't handle non-finite values.
Results may differ from a plain program's by a relative error of at most 0.0029.
Values sent between devices are 32-bit elements; how exact they have to be, the bound alone decides.
No kernel may reach another device: no remote copies, remote signals or barrier semaphores. Data moves between devices by JAX's collectives and lax.ppermute only.
A program may use at most 192 MiB of HBM per device.

v0:
```python
import functools

import jax
import jax.numpy as jnp
from jax import lax
from jax.experimental import pallas as pl
from jax.experimental.pallas import tpu as pltpu
from jax.sharding import PartitionSpec as P


BAND = 4
BPO = 24
PAIRS = ((0, 0), (1, 1), (2, 2), (0, 1), (0, 2), (1, 2))
ROWS = 32
HEAD = 6 * ROWS
PKT = HEAD + 8
STEP = 1024


F32 = jnp.float32
VMEM = pl.BlockSpec(memory_space=pltpu.VMEM)
SMEM = pl.BlockSpec(memory_space=pltpu.SMEM)
ANY = pl.BlockSpec(memory_space=pl.ANY)
HBM = pl.BlockSpec(memory_space=pltpu.HBM)


def write_packets(s, total, map_ref, outs):
    me = lax.axis_index("col")
    for d, out in enumerate(outs):
        lane = lax.rem(me + d, 4)
        for p, (i, j) in enumerate(PAIRS):
            rows = pl.ds(pl.multiple_of(i * 128 + lane * ROWS, ROWS), ROWS)
            out[s, p * ROWS : (p + 1) * ROWS, :] = total[rows, j * 128 : (j + 1) * 128]
    if map_ref is not None:
        first = map_ref[s, 0]
        code = (first * 4 + map_ref[s, 1] - first) * 4 + map_ref[s, 2] - first
        head = jnp.full((8, 128), code.astype(F32), F32)
        for out in outs:
            out[s, HEAD:PKT, :] = head


def k_kernel(map_ref, bb, bi, cm, o0, o1, o2, o3, total):
    for i in range(3):
        total[i * 128 : (i + 1) * 128, :] = bb[0, i].astype(F32)
    total[0:128, :] += jnp.dot(bi[0, 0:128, :], cm[0], preferred_element_type=F32)
    total[128:384, 128:384] += jnp.dot(
        bi[0, 128:384, :], cm[0, :, 128:384], preferred_element_type=F32
    )
    write_packets(pl.program_id(0), total, map_ref, (o0, o1, o2, o3))


def k_packets(bmap, stiff_bb, stiff_bi, cm):
    count, order, inner = stiff_bi.shape
    return pl.pallas_call(
        k_kernel,
        grid=(count,),
        in_specs=[
            SMEM,
            pl.BlockSpec((1, 3, 128, order), lambda s: (s, 0, 0, 0)),
            pl.BlockSpec((1, order, inner), lambda s: (s, 0, 0)),
            pl.BlockSpec((1, inner, order), lambda s: (s, 0, 0)),
        ],
        out_specs=[VMEM] * 4,
        out_shape=[held(count, PKT)] * 4,
        scratch_shapes=[pltpu.VMEM((order, order), F32)],
        compiler_params=pltpu.CompilerParams(vmem_limit_bytes=56 << 20),
        cost_estimate=pl.CostEstimate(
            flops=6 * count * 128 * 128 * inner * 2, bytes_accessed=16000000, transcendentals=0
        ),
        name="stiffness",
    )(bmap, stiff_bb, stiff_bi, cm)


def m_kernel(steps, bb, im, cm, fm, o0, o1, o2, o3, coup, total, w):
    s, k = pl.program_id(0), pl.program_id(1)

    @pl.when(k == 0)
    def _():
        for i in range(3):
            total[i * 128 : (i + 1) * 128, :] = bb[0, i].astype(F32)
        coup[...] = jnp.zeros_like(coup)

    for j in range(STEP // 128):
        lines = im[:, pl.ds(pl.multiple_of(k * STEP + j * 128, 128), 128)]
        mine = lax.broadcasted_iota(jnp.int32, lines.shape, 0) == s
        line = jnp.sum(jnp.where(mine, lines, 0.0), axis=0, keepdims=True)
        column = jnp.broadcast_to(line, (128, 128)).T
        part = slice(j * 128, (j + 1) * 128)
        for i in range(3):
            lanes = slice(i * 128, (i + 1) * 128)
            w[part, lanes] = (column * cm[0, part, lanes].astype(F32)).astype(jnp.bfloat16)
    dims = (((0,), (0,)), ((), ()))
    total[0:128, :] += lax.dot_general(cm[0, :, 0:128], w[...], dims, preferred_element_type=F32)
    total[128:384, 128:384] += lax.dot_general(
        cm[0, :, 128:384], w[:, 128:384], dims, preferred_element_type=F32
    )
    coup[0] += lax.dot_general(fm[0], w[...], dims, preferred_element_type=F32)

    @pl.when(k == steps - 1)
    def _():
        write_packets(s, total, None, (o0, o1, o2, o3))


def m_packets(mass_bb, im, cm, fm):
    count, inner, order = cm.shape
    modes = fm.shape[2]
    steps = inner // STEP
    return pl.pallas_call(
        functools.partial(m_kernel, steps),
        grid=(count, steps),
        in_specs=[
            pl.BlockSpec((1, 3, 128, order), lambda s, k: (s, 0, 0, 0)),
            pl.BlockSpec((count, inner), lambda s, k: (0, 0)),
            pl.BlockSpec((1, STEP, order), lambda s, k: (s, k, 0)),
            pl.BlockSpec((1, STEP, modes), lambda s, k: (s, k, 0)),
        ],
        compiler_params=pltpu.CompilerParams(vmem_limit_bytes=52 << 20),
        out_specs=[VMEM] * 4
        + [pl.BlockSpec((1, modes, order), lambda s, k: (s, 0, 0))],
        out_shape=[held(count, HEAD)] * 4 + [jax.ShapeDtypeStruct((count, modes, order), F32)],
        scratch_shapes=[pltpu.VMEM((order, order), F32), pltpu.VMEM((STEP, order), jnp.bfloat16)],
        cost_estimate=pl.CostEstimate(
            flops=12 * count * 128 * 128 * inner * 2, bytes_accessed=14000000, transcendentals=0
        ),
        name="mass",
    )(mass_bb, im, cm, fm)


SMALL = pltpu.CompilerParams(vmem_limit_bytes=4 << 20)


def near(bufs):
    return [pltpu.with_memory_space_constraint(buf, pltpu.VMEM) for buf in bufs]


def held(count, rows):
    return pltpu.VMEM((count, rows, 128), F32)


def codes_of(slots):
    return [jnp.max(ref[n, HEAD : HEAD + 1, :]).astype(jnp.int32) for ref, n in slots]


def place():
    r = lax.axis_index("row")
    core = lax.rem(r, 2)
    x = lax.rem(r // 2, 4)
    y = r // 8
    u = jnp.where(core == 0, x, y)
    v = jnp.where(core == 0, y, x)
    return core, u, v


def pack_kernel(*refs):
    keys, ins, outs = refs[:4], refs[-8:-4], refs[-4:]
    core, u, v = place()
    if outs[0].shape[1] == PKT:
        empty = jnp.full((8, 128), -1.0, F32)
        for out in outs:
            for n in range(8):
                out[n, HEAD:PKT, :] = empty
    count = ins[0].shape[0]
    codes = codes_of([(ref, n) for ref in keys for n in range(count)])
    for n, code in enumerate(codes):
        owner = code // (BPO * 16)
        c = lax.rem(owner, 2)
        x = lax.rem(owner // 2, 4)
        y = owner // 8
        du = lax.rem(jnp.where(core == 0, x, y) - u + 4, 4)
        dv = lax.rem(jnp.where(core == 0, y, x) - v + 4, 4)
        slot = dv * 2 + lax.rem(c + core, 2)
        for k, out in enumerate(outs):

            @pl.when(du == k)
            def _(out=out, n=n, slot=slot):
                out[slot] = ins[n // count][n % count]


def pack(keys, bufs):
    bufs = keys if bufs is None else keys + bufs
    return pl.pallas_call(
        pack_kernel,
        in_specs=[VMEM] * len(bufs),
        out_specs=[VMEM] * 4,
        out_shape=[held(8, bufs[-1].shape[1])] * 4,
        compiler_params=SMALL,
        cost_estimate=pl.CostEstimate(flops=2000000, bytes_accessed=4000000, transcendentals=0),
        name="pack",
    )(*near(bufs))


def turn_kernel(*refs):
    ins, outs = refs[:4], refs[4:]
    for k in range(4):
        for q in range(1, 8):
            outs[q - 1][k] = ins[k][q]


def turn(bufs):
    return pl.pallas_call(
        turn_kernel,
        in_specs=[VMEM] * 4,
        out_specs=[VMEM] * 7,
        out_shape=[held(4, bufs[0].shape[1])] * 7,
        compiler_params=SMALL,
        cost_estimate=pl.CostEstimate(flops=2000000, bytes_accessed=6000000, transcendentals=0),
        name="turn",
    )(*near(bufs))


def sum_kernel(*refs):
    keys, ins, band = refs[:11], refs[-12:-1], refs[-1]

    def slots(some):
        return [(ref, 0) for ref in some[:4]] + [(ref, n) for ref in some[4:] for n in range(4)]

    codes = codes_of(slots(keys))
    band[...] = jnp.zeros_like(band)
    for (ref, n), code in zip(slots(ins), codes):

        @pl.when(code >= 0)
        def _(ref=ref, n=n, code=code):
            last = lax.rem(code, 4)
            mid = lax.rem(code // 4, 4)
            base = lax.rem(code // 16, BPO)
            marks = (0, mid, last)
            for p, (i, j) in enumerate(PAIRS):
                g = base + marks[i]
                d = marks[j] - marks[i]
                band[g, d] += ref[n, p * ROWS : (p + 1) * ROWS, :]


def assemble(keys, bufs):
    bufs = keys if bufs is None else keys + bufs
    return pl.pallas_call(
        sum_kernel,
        in_specs=[VMEM] * len(bufs),
        out_specs=VMEM,
        out_shape=jax.ShapeDtypeStruct((BPO, BAND, ROWS, 128), F32),
        compiler_params=SMALL,
        cost_estimate=pl.CostEstimate(flops=4000000, bytes_accessed=6000000, transcendentals=0),
        name="assemble",
    )(*near(bufs))


def spots():
    return [(r // 8, (r // 2) % 4, r % 2) for r in range(32)]


def row_of(y, x, c):
    return (y % 4) * 8 + (x % 4) * 2 + c


def first_turn(d):
    return [
        (r, row_of(y, x + d, c) if c == 0 else row_of(y + d, x, c))
        for r, (y, x, c) in enumerate(spots())
    ]


def second_turn(d, e):
    return [
        (r, row_of(y + d, x, c ^ e) if c == 0 else row_of(y, x + d, c ^ e))
        for r, (y, x, c) in enumerate(spots())
    ]


def over_col(bufs):
    return [bufs[0]] + [
        lax.ppermute(bufs[d], "col", [(z, (z + d) % 4) for z in range(4)]) for d in (1, 2, 3)
    ]


def over_u(keys, bufs):
    slots = pack(keys, bufs)
    two = lax.ppermute(slots[2], "row", first_turn(2))
    one = lax.ppermute(slots[1], "row", first_turn(1))
    three = lax.ppermute(slots[3], "row", first_turn(3))
    return [slots[0], one, two, three]


def over_v(slots):
    parts = turn(slots)
    return slots + [
        lax.ppermute(parts[q - 1], "row", second_turn(q // 2, q % 2))
        for q in (4, 2, 6, 5, 3, 7, 1)
    ]


def per_device(
    stiff_bb, stiff_bi, constraint_modes, interior_mass, fixed_modes, mass_bb, boundary_map
):
    k_out = k_packets(boundary_map, stiff_bb, stiff_bi, constraint_modes)
    k_in = over_col(k_out)
    *m_out, coupling = m_packets(mass_bb, interior_mass, constraint_modes, fixed_modes)
    m_in = over_col(m_out)
    k_half = over_u(k_in, None)
    m_half = over_u(k_in, m_in)
    k_end = over_v(k_half)
    m_end = over_v(m_half)
    band_k = assemble(k_end, None)
    band_m = assemble(k_end, m_end)
    return band_k, band_m, coupling


def solution(mesh):
    placed = (
        P(("row", "col"), None, None, None),
        P(("row", "col"), None, None),
        P(("row", "col"), None, None),
        P(("row", "col"), None),
        P(("row", "col"), None, None),
        P(("row", "col"), None, None, None),
        P(("row", "col"), None),
    )
    return jax.shard_map(
        per_device,
        mesh=mesh,
        in_specs=placed,
        out_specs=(
            P("row", None, "col", None),
            P("row", None, "col", None),
            P(("row", "col"), None, None),
        ),
        check_vma=False,
    )
```

profile of v0, /device:TPU:0, one launch (start us, length us, event | category | flops | bytes accessed | tf_op | source)
XLA Modules:
  0.0 128.2 jit_solution(7820899864538059343)
XLA Ops:
  0.6 0.0 copy-start
  0.6 7.1 %stiffness.1 = (f32[3,200,128]{2,1,0:T(8,128)S(1)}, f32[3,200,128]{2,1,0:T(8,128)S(1)}, f32[3,200,128]{2,1,0:T(8,128)S(1)}, f32[3,200,128]{2,1,0:T(8,128)S(1)}) custom-call(s32[3,3]{1,0:T(4,128)} %map_ref.1, bf16[3,3,128,384]{3,2,1,0:T(8,128)(2,1)} %bb.2, bf16[3,384,3072]{2,1,0:T(8,128)(2,1)} %bi.1, bf16[3,3072,384]{2,1,0:T(8,128)(2,1)} %cm.3), custom_call_target="tpu_custom_call" | custom-call | flops 1811939328 | bytes 16000000 | tf_op jit(solution)/shard_map/stiffness/pallas_call | solution.py:54
  7.8 2.1 %collective-permute-start = (f32[3,200,128]{2,1,0:T(8,128)S(1)}, f32[3,200,128]{2,1,0:T(8,128)S(1)}, u32[]{:S(2)}, u32[]{:S(2)}) collective-permute-start(f32[3,200,128]{2,1,0:T(8,128)S(1)} %get-tuple-element.35), channel_id=1, source_target_pairs={{0,1},{1,2},{2,3},{3,0},{4,5},{5,6},{6,7},{7,4},{8,9},{9,10},{10,1... | collective-permute-start | bytes 921608 | tf_op jit(solution)/shard_map/ppermute | solution.py:270
  9.9 3.6 %collective-permute-start.1 = (f32[3,200,128]{2,1,0:T(8,128)S(1)}, f32[3,200,128]{2,1,0:T(8,128)S(1)}, u32[]{:S(2)}, u32[]{:S(2)}) collective-permute-start(f32[3,200,128]{2,1,0:T(8,128)S(1)} %get-tuple-element.36), channel_id=1, source_target_pairs={{0,2},{1,3},{2,0},{3,1},{4,6},{5,7},{6,4},{7,5},{8,10},{9,11},{10,... | collective-permute-start | bytes 921608 | tf_op jit(solution)/shard_map/ppermute | solution.py:270
  13.4 1.0 collective-permute-start.2
  14.4 4.8 %collective-permute-done.refs_1_ = f32[3,200,128]{2,1,0:T(8,128)S(1)} collective-permute-done((f32[3,200,128]{2,1,0:T(8,128)S(1)}, f32[3,200,128]{2,1,0:T(8,128)S(1)}, u32[]{:S(2)}, u32[]{:S(2)}) %collective-permute-start) | collective-permute-done | bytes 307232 | tf_op jit(solution)/shard_map/ppermute | solution.py:270
  19.2 7.8 %collective-permute-done.1.refs_2_ = f32[3,200,128]{2,1,0:T(8,128)S(1)} collective-permute-done((f32[3,200,128]{2,1,0:T(8,128)S(1)}, f32[3,200,128]{2,1,0:T(8,128)S(1)}, u32[]{:S(2)}, u32[]{:S(2)}) %collective-permute-start.1) | collective-permute-done | bytes 307232 | tf_op jit(solution)/shard_map/ppermute | solution.py:270
  27.0 0.0 collective-permute-done.2.refs_3_
  27.0 0.8 pack.2
  27.8 1.6 %collective-permute-start.3 = (f32[8,200,128]{2,1,0:T(8,128)S(1)}, f32[8,200,128]{2,1,0:T(8,128)S(1)}, u32[]{:S(2)}, u32[]{:S(2)}) collective-permute-start(f32[8,200,128]{2,1,0:T(8,128)S(1)} %get-tuple-element.39), channel_id=1, source_target_pairs={{0,8},{4,36},{8,16},{12,44},{16,24},{20,52},{24,0},{28,60},{32,40}... | collective-permute-start | bytes 2457608 | tf_op jit(solution)/shard_map/ppermute | solution.py:277
  29.3 0.0 copy-done
  29.3 12.9 %mass.1 = (f32[3,192,128]{2,1,0:T(8,128)S(1)}, f32[3,192,128]{2,1,0:T(8,128)S(1)}, f32[3,192,128]{2,1,0:T(8,128)S(1)}, f32[3,192,128]{2,1,0:T(8,128)S(1)}, f32[3,256,384]{2,1,0:T(8,128)}) custom-call(bf16[3,3,128,384]{3,2,1,0:T(8,128)(2,1)} %bb.3, f32[3,3072]{1,0:T(4,128)S(1)} %copy-done, bf16[3,3072,384]{2,1,0:T(8,128)(2,1)} %cm.3, bf16[3,3072,256]{2,1,0:T(8,128)(2,1)} %fm.1), custom_call_target="tpu_custom_call" | custom-call | flops 3623878656 | bytes 14000000 | tf_op jit(solution)/shard_map/mass/pallas_call | solution.py:108
  42.2 1.2 collective-permute-start.13
  43.5 2.4 %collective-permute-start.14 = (f32[3,192,128]{2,1,0:T(8,128)S(1)}, f32[3,192,128]{2,1,0:T(8,128)S(1)}, u32[]{:S(2)}, u32[]{:S(2)}) collective-permute-start(f32[3,192,128]{2,1,0:T(8,128)S(1)} %get-tuple-element.51), channel_id=1, source_target_pairs={{0,2},{1,3},{2,0},{3,1},{4,6},{5,7},{6,4},{7,5},{8,10},{9,11},{10,... | collective-permute-start | bytes 884744 | tf_op jit(solution)/shard_map/ppermute | solution.py:270
  45.9 1.2 collective-permute-start.15
  47.1 2.7 %collective-permute-start.4 = (f32[8,200,128]{2,1,0:T(8,128)S(1)}, f32[8,200,128]{2,1,0:T(8,128)S(1)}, u32[]{:S(2)}, u32[]{:S(2)}) collective-permute-start(f32[8,200,128]{2,1,0:T(8,128)S(1)} %get-tuple-element.40), channel_id=1, source_target_pairs={{0,16},{4,68},{8,24},{12,76},{16,0},{20,84},{24,8},{28,92},{32,48}... | collective-permute-start | bytes 2457608 | tf_op jit(solution)/shard_map/ppermute | solution.py:276
  49.8 1.6 %collective-permute-done.13.refs_5_ = f32[3,192,128]{2,1,0:T(8,128)S(1)} collective-permute-done((f32[3,192,128]{2,1,0:T(8,128)S(1)}, f32[3,192,128]{2,1,0:T(8,128)S(1)}, u32[]{:S(2)}, u32[]{:S(2)}) %collective-permute-start.13) | collective-permute-done | bytes 294944 | tf_op jit(solution)/shard_map/ppermute | solution.py:270
  51.4 2.8 %collective-permute-start.5 = (f32[8,200,128]{2,1,0:T(8,128)S(1)}, f32[8,200,128]{2,1,0:T(8,128)S(1)}, u32[]{:S(2)}, u32[]{:S(2)}) collective-permute-start(f32[8,200,128]{2,1,0:T(8,128)S(1)} %get-tuple-element.41), channel_id=1, source_target_pairs={{0,24},{4,100},{8,0},{12,108},{16,8},{20,116},{24,16},{28,124},{32... | collective-permute-start | bytes 2457608 | tf_op jit(solution)/shard_map/ppermute | solution.py:278
  54.1 4.7 %collective-permute-done.14.refs_6_ = f32[3,192,128]{2,1,0:T(8,128)S(1)} collective-permute-done((f32[3,192,128]{2,1,0:T(8,128)S(1)}, f32[3,192,128]{2,1,0:T(8,128)S(1)}, u32[]{:S(2)}, u32[]{:S(2)}) %collective-permute-start.14) | collective-permute-done | bytes 294944 | tf_op jit(solution)/shard_map/ppermute | solution.py:270
  58.9 0.0 collective-permute-done.15.refs_7_
  58.9 0.8 pack.3
  59.6 1.6 %collective-permute-start.16 = (f32[8,192,128]{2,1,0:T(8,128)S(1)}, f32[8,192,128]{2,1,0:T(8,128)S(1)}, u32[]{:S(2)}, u32[]{:S(2)}) collective-permute-start(f32[8,192,128]{2,1,0:T(8,128)S(1)} %get-tuple-element.54), channel_id=1, source_target_pairs={{0,8},{4,36},{8,16},{12,44},{16,24},{20,52},{24,0},{28,60},{32,40}... | collective-permute-start | bytes 2359304 | tf_op jit(solution)/shard_map/ppermute | solution.py:277
  61.2 2.7 %collective-permute-start.17 = (f32[8,192,128]{2,1,0:T(8,128)S(1)}, f32[8,192,128]{2,1,0:T(8,128)S(1)}, u32[]{:S(2)}, u32[]{:S(2)}) collective-permute-start(f32[8,192,128]{2,1,0:T(8,128)S(1)} %get-tuple-element.55), channel_id=1, source_target_pairs={{0,16},{4,68},{8,24},{12,76},{16,0},{20,84},{24,8},{28,92},{32,48}... | collective-permute-start | bytes 2359304 | tf_op jit(solution)/shard_map/ppermute | solution.py:276
  63.9 0.0 collective-permute-done.3.refs_1_
  63.9 1.4 %collective-permute-start.18 = (f32[8,192,128]{2,1,0:T(8,128)S(1)}, f32[8,192,128]{2,1,0:T(8,128)S(1)}, u32[]{:S(2)}, u32[]{:S(2)}) collective-permute-start(f32[8,192,128]{2,1,0:T(8,128)S(1)} %get-tuple-element.56), channel_id=1, source_target_pairs={{0,24},{4,100},{8,0},{12,108},{16,8},{20,116},{24,16},{28,124},{32... | collective-permute-start | bytes 2359304 | tf_op jit(solution)/shard_map/ppermute | solution.py:278
  65.4 0.0 collective-permute-done.4.refs_2_
  65.4 3.5 %collective-permute-done.5.refs_3_ = f32[8,200,128]{2,1,0:T(8,128)S(1)} collective-permute-done((f32[8,200,128]{2,1,0:T(8,128)S(1)}, f32[8,200,128]{2,1,0:T(8,128)S(1)}, u32[]{:S(2)}, u32[]{:S(2)}) %collective-permute-start.5) | collective-permute-done | bytes 819232 | tf_op jit(solution)/shard_map/ppermute | solution.py:278
  68.8 0.2 turn.2
  69.0 3.3 %collective-permute-start.6 = (f32[4,200,128]{2,1,0:T(8,128)S(1)}, f32[4,200,128]{2,1,0:T(8,128)S(1)}, u32[]{:S(2)}, u32[]{:S(2)}) collective-permute-start(f32[4,200,128]{2,1,0:T(8,128)S(1)} %get-tuple-element.42), channel_id=1, source_target_pairs={{0,64},{4,20},{8,72},{12,28},{16,80},{20,4},{24,88},{28,12},{32,96... | collective-permute-start | bytes 1228808 | tf_op jit(solution)/shard_map/ppermute | solution.py:285
  72.3 0.7 collective-permute-start.7
  73.0 6.8 %collective-permute-done.16.refs_1_.refs_12_ = f32[8,192,128]{2,1,0:T(8,128)S(1)} collective-permute-done((f32[8,192,128]{2,1,0:T(8,128)S(1)}, f32[8,192,128]{2,1,0:T(8,128)S(1)}, u32[]{:S(2)}, u32[]{:S(2)}) %collective-permute-start.16) | collective-permute-done | bytes 786464 | tf_op jit(solution)/shard_map/ppermute | solution.py:277
  79.7 11.4 %collective-permute-done.17.refs_2_.refs_13_ = f32[8,192,128]{2,1,0:T(8,128)S(1)} collective-permute-done((f32[8,192,128]{2,1,0:T(8,128)S(1)}, f32[8,192,128]{2,1,0:T(8,128)S(1)}, u32[]{:S(2)}, u32[]{:S(2)}) %collective-permute-start.17) | collective-permute-done | bytes 786464 | tf_op jit(solution)/shard_map/ppermute | solution.py:276
  91.2 0.0 collective-permute-done.18.refs_3_.refs_14_
  91.2 0.2 turn.3
  91.3 3.0 %collective-permute-start.19 = (f32[4,192,128]{2,1,0:T(8,128)S(1)}, f32[4,192,128]{2,1,0:T(8,128)S(1)}, u32[]{:S(2)}, u32[]{:S(2)}) collective-permute-start(f32[4,192,128]{2,1,0:T(8,128)S(1)} %get-tuple-element.57), channel_id=1, source_target_pairs={{0,64},{4,20},{8,72},{12,28},{16,80},{20,4},{24,88},{28,12},{32,96... | collective-permute-start | bytes 1179656 | tf_op jit(solution)/shard_map/ppermute | solution.py:285
  94.3 0.0 collective-permute-start.20
  94.3 3.2 %collective-permute-start.8 = (f32[4,200,128]{2,1,0:T(8,128)S(1)}, f32[4,200,128]{2,1,0:T(8,128)S(1)}, u32[]{:S(2)}, u32[]{:S(2)}) collective-permute-start(f32[4,200,128]{2,1,0:T(8,128)S(1)} %get-tuple-element.44), channel_id=1, source_target_pairs={{0,96},{4,28},{8,104},{12,4},{16,112},{20,12},{24,120},{28,20},{32... | collective-permute-start | bytes 1228808 | tf_op jit(solution)/shard_map/ppermute | solution.py:285
  97.6 3.2 %collective-permute-done.19.refs_15_ = f32[4,192,128]{2,1,0:T(8,128)S(1)} collective-permute-done((f32[4,192,128]{2,1,0:T(8,128)S(1)}, f32[4,192,128]{2,1,0:T(8,128)S(1)}, u32[]{:S(2)}, u32[]{:S(2)}) %collective-permute-start.19) | collective-permute-done | bytes 393248 | tf_op jit(solution)/shard_map/ppermute | solution.py:285
  100.8 0.0 collective-permute-start.9
  100.8 4.1 %collective-permute-done.20.refs_16_ = f32[4,192,128]{2,1,0:T(8,128)S(1)} collective-permute-done((f32[4,192,128]{2,1,0:T(8,128)S(1)}, f32[4,192,128]{2,1,0:T(8,128)S(1)}, u32[]{:S(2)}, u32[]{:S(2)}) %collective-permute-start.20) | collective-permute-done | bytes 393248 | tf_op jit(solution)/shard_map/ppermute | solution.py:285
  104.9 0.0 collective-permute-start.10
  104.9 0.0 collective-permute-done.6.refs_4_
  104.9 1.6 %collective-permute-start.11 = (f32[4,200,128]{2,1,0:T(8,128)S(1)}, f32[4,200,128]{2,1,0:T(8,128)S(1)}, u32[]{:S(2)}, u32[]{:S(2)}) collective-permute-start(f32[4,200,128]{2,1,0:T(8,128)S(1)} %get-tuple-element.47), channel_id=1, source_target_pairs={{0,100},{4,24},{8,108},{12,0},{16,116},{20,8},{24,124},{28,16},{32... | collective-permute-start | bytes 1228808 | tf_op jit(solution)/shard_map/ppermute | solution.py:285
  106.5 0.0 collective-permute-done.7.refs_5_
  106.5 0.1 collective-permute-start.12
  106.6 0.0 collective-permute-done.8.refs_6_
  106.6 2.4 %collective-permute-start.21 = (f32[4,192,128]{2,1,0:T(8,128)S(1)}, f32[4,192,128]{2,1,0:T(8,128)S(1)}, u32[]{:S(2)}, u32[]{:S(2)}) collective-permute-start(f32[4,192,128]{2,1,0:T(8,128)S(1)} %get-tuple-element.59), channel_id=1, source_target_pairs={{0,96},{4,28},{8,104},{12,4},{16,112},{20,12},{24,120},{28,20},{32... | collective-permute-start | bytes 1179656 | tf_op jit(solution)/shard_map/ppermute | solution.py:285
  109.0 0.7 collective-permute-done.9.refs_7_
  109.7 2.3 %collective-permute-start.22 = (f32[4,192,128]{2,1,0:T(8,128)S(1)}, f32[4,192,128]{2,1,0:T(8,128)S(1)}, u32[]{:S(2)}, u32[]{:S(2)}) collective-permute-start(f32[4,192,128]{2,1,0:T(8,128)S(1)} %get-tuple-element.60), channel_id=1, source_target_pairs={{0,68},{4,16},{8,76},{12,24},{16,84},{20,0},{24,92},{28,8},{32,100... | collective-permute-start | bytes 1179656 | tf_op jit(solution)/shard_map/ppermute | solution.py:285
  112.0 2.1 %collective-permute-done.10.refs_8_ = f32[4,200,128]{2,1,0:T(8,128)S(1)} collective-permute-done((f32[4,200,128]{2,1,0:T(8,128)S(1)}, f32[4,200,128]{2,1,0:T(8,128)S(1)}, u32[]{:S(2)}, u32[]{:S(2)}) %collective-permute-start.10) | collective-permute-done | bytes 409632 | tf_op jit(solution)/shard_map/ppermute | solution.py:285
  114.1 0.8 collective-permute-start.23
  114.9 0.0 collective-permute-done.11.refs_9_
  114.9 2.5 %collective-permute-start.24 = (f32[4,192,128]{2,1,0:T(8,128)S(1)}, f32[4,192,128]{2,1,0:T(8,128)S(1)}, u32[]{:S(2)}, u32[]{:S(2)}) collective-permute-start(f32[4,192,128]{2,1,0:T(8,128)S(1)} %get-tuple-element.62), channel_id=1, source_target_pairs={{0,100},{4,24},{8,108},{12,0},{16,116},{20,8},{24,124},{28,16},{32... | collective-permute-start | bytes 1179656 | tf_op jit(solution)/shard_map/ppermute | solution.py:285
  117.4 0.0 collective-permute-done.12.refs_10_
  117.4 0.0 collective-permute-start.25
  117.4 2.5 %assemble.2 = f32[24,4,32,128]{3,2,1,0:T(8,128)} custom-call(f32[8,200,128]{2,1,0:T(8,128)S(1)} %get-tuple-element.38.refs_0_, f32[8,200,128]{2,1,0:T(8,128)S(1)} %collective-permute-done.3.refs_1_, f32[8,200,128]{2,1,0:T(8,128)S(1)} %collective-permute-done.4.refs_2_, f32[8,200,128]{2,1,0:T(8,128)S(1)} %collective-permute-done.5.refs_3_, ...), custom_call_target="tpu_custom_call" | custom-call | flops 4000000 | bytes 6000000 | tf_op jit(solution)/shard_map/assemble/pallas_call | solution.py:235
  120.0 0.0 collective-permute-done.21.refs_17_
  120.0 0.0 collective-permute-done.22.refs_18_
  120.0 2.7 %collective-permute-done.23.refs_19_ = f32[4,192,128]{2,1,0:T(8,128)S(1)} collective-permute-done((f32[4,192,128]{2,1,0:T(8,128)S(1)}, f32[4,192,128]{2,1,0:T(8,128)S(1)}, u32[]{:S(2)}, u32[]{:S(2)}) %collective-permute-start.23) | collective-permute-done | bytes 393248 | tf_op jit(solution)/shard_map/ppermute | solution.py:285
  122.7 3.0 %collective-permute-done.24.refs_20_ = f32[4,192,128]{2,1,0:T(8,128)S(1)} collective-permute-done((f32[4,192,128]{2,1,0:T(8,128)S(1)}, f32[4,192,128]{2,1,0:T(8,128)S(1)}, u32[]{:S(2)}, u32[]{:S(2)}) %collective-permute-start.24) | collective-permute-done | bytes 393248 | tf_op jit(solution)/shard_map/ppermute | solution.py:285
  125.6 0.0 collective-permute-done.25.refs_21_
  125.6 2.5 %assemble.3 = f32[24,4,32,128]{3,2,1,0:T(8,128)} custom-call(f32[8,200,128]{2,1,0:T(8,128)S(1)} %get-tuple-element.38.refs_0_, f32[8,200,128]{2,1,0:T(8,128)S(1)} %collective-permute-done.3.refs_1_, f32[8,200,128]{2,1,0:T(8,128)S(1)} %collective-permute-done.4.refs_2_, f32[8,200,128]{2,1,0:T(8,128)S(1)} %collective-permute-done.5.refs_3_, ...), custom_call_target="tpu_custom_call" | custom-call | flops 4000000 | bytes 6000000 | tf_op jit(solution)/shard_map/assemble/pallas_call | solution.py:235
Async XLA Ops:
  0.6 28.7 %copy-start = (f32[3,3072]{1,0:T(4,128)S(1)}, f32[3,3072]{1,0:T(4,128)}, u32[]{:S(2)}) copy-start(f32[3,3072]{1,0:T(4,128)} %im.1) | copy-start | bytes 110596
  7.8 11.5 %collective-permute-start = (f32[3,200,128]{2,1,0:T(8,128)S(1)}, f32[3,200,128]{2,1,0:T(8,128)S(1)}, u32[]{:S(2)}, u32[]{:S(2)}) collective-permute-start(f32[3,200,128]{2,1,0:T(8,128)S(1)} %get-tuple-element.35), channel_id=1, source_target_pairs={{0,1},{1,2},{2,3},{3,0},{4,5},{5,6},{6,7},{7,4},{8,9},{9,10},{10,1... | collective-permute-start | bytes 921608 | tf_op jit(solution)/shard_map/ppermute | solution.py:270
  9.9 17.2 %collective-permute-start.1 = (f32[3,200,128]{2,1,0:T(8,128)S(1)}, f32[3,200,128]{2,1,0:T(8,128)S(1)}, u32[]{:S(2)}, u32[]{:S(2)}) collective-permute-start(f32[3,200,128]{2,1,0:T(8,128)S(1)} %get-tuple-element.36), channel_id=1, source_target_pairs={{0,2},{1,3},{2,0},{3,1},{4,6},{5,7},{6,4},{7,5},{8,10},{9,11},{10,... | collective-permute-start | bytes 921608 | tf_op jit(solution)/shard_map/ppermute | solution.py:270
  13.4 13.6 %collective-permute-start.2 = (f32[3,200,128]{2,1,0:T(8,128)S(1)}, f32[3,200,128]{2,1,0:T(8,128)S(1)}, u32[]{:S(2)}, u32[]{:S(2)}) collective-permute-start(f32[3,200,128]{2,1,0:T(8,128)S(1)} %get-tuple-element.37), channel_id=1, source_target_pairs={{0,3},{1,0},{2,1},{3,2},{4,7},{5,4},{6,5},{7,6},{8,11},{9,8},{10,9... | collective-permute-start | bytes 921608 | tf_op jit(solution)/shard_map/ppermute | solution.py:270
  27.8 36.2 %collective-permute-start.3 = (f32[8,200,128]{2,1,0:T(8,128)S(1)}, f32[8,200,128]{2,1,0:T(8,128)S(1)}, u32[]{:S(2)}, u32[]{:S(2)}) collective-permute-start(f32[8,200,128]{2,1,0:T(8,128)S(1)} %get-tuple-element.39), channel_id=1, source_target_pairs={{0,8},{4,36},{8,16},{12,44},{16,24},{20,52},{24,0},{28,60},{32,40}... | collective-permute-start | bytes 2457608 | tf_op jit(solution)/shard_map/ppermute | solution.py:277
  42.2 9.1 %collective-permute-start.13 = (f32[3,192,128]{2,1,0:T(8,128)S(1)}, f32[3,192,128]{2,1,0:T(8,128)S(1)}, u32[]{:S(2)}, u32[]{:S(2)}) collective-permute-start(f32[3,192,128]{2,1,0:T(8,128)S(1)} %get-tuple-element.50), channel_id=1, source_target_pairs={{0,1},{1,2},{2,3},{3,0},{4,5},{5,6},{6,7},{7,4},{8,9},{9,10},{10,1... | collective-permute-start | bytes 884744 | tf_op jit(solution)/shard_map/ppermute | solution.py:270
  43.5 15.4 %collective-permute-start.14 = (f32[3,192,128]{2,1,0:T(8,128)S(1)}, f32[3,192,128]{2,1,0:T(8,128)S(1)}, u32[]{:S(2)}, u32[]{:S(2)}) collective-permute-start(f32[3,192,128]{2,1,0:T(8,128)S(1)} %get-tuple-element.51), channel_id=1, source_target_pairs={{0,2},{1,3},{2,0},{3,1},{4,6},{5,7},{6,4},{7,5},{8,10},{9,11},{10,... | collective-permute-start | bytes 884744 | tf_op jit(solution)/shard_map/ppermute | solution.py:270
  45.9 13.0 %collective-permute-start.15 = (f32[3,192,128]{2,1,0:T(8,128)S(1)}, f32[3,192,128]{2,1,0:T(8,128)S(1)}, u32[]{:S(2)}, u32[]{:S(2)}) collective-permute-start(f32[3,192,128]{2,1,0:T(8,128)S(1)} %get-tuple-element.52), channel_id=1, source_target_pairs={{0,3},{1,0},{2,1},{3,2},{4,7},{5,4},{6,5},{7,6},{8,11},{9,8},{10,9... | collective-permute-start | bytes 884744 | tf_op jit(solution)/shard_map/ppermute | solution.py:270
  47.1 18.3 %collective-permute-start.4 = (f32[8,200,128]{2,1,0:T(8,128)S(1)}, f32[8,200,128]{2,1,0:T(8,128)S(1)}, u32[]{:S(2)}, u32[]{:S(2)}) collective-permute-start(f32[8,200,128]{2,1,0:T(8,128)S(1)} %get-tuple-element.40), channel_id=1, source_target_pairs={{0,16},{4,68},{8,24},{12,76},{16,0},{20,84},{24,8},{28,92},{32,48}... | collective-permute-start | bytes 2457608 | tf_op jit(solution)/shard_map/ppermute | solution.py:276
  51.4 17.5 %collective-permute-start.5 = (f32[8,200,128]{2,1,0:T(8,128)S(1)}, f32[8,200,128]{2,1,0:T(8,128)S(1)}, u32[]{:S(2)}, u32[]{:S(2)}) collective-permute-start(f32[8,200,128]{2,1,0:T(8,128)S(1)} %get-tuple-element.41), channel_id=1, source_target_pairs={{0,24},{4,100},{8,0},{12,108},{16,8},{20,116},{24,16},{28,124},{32... | collective-permute-start | bytes 2457608 | tf_op jit(solution)/shard_map/ppermute | solution.py:278
  59.6 20.1 %collective-permute-start.16 = (f32[8,192,128]{2,1,0:T(8,128)S(1)}, f32[8,192,128]{2,1,0:T(8,128)S(1)}, u32[]{:S(2)}, u32[]{:S(2)}) collective-permute-start(f32[8,192,128]{2,1,0:T(8,128)S(1)} %get-tuple-element.54), channel_id=1, source_target_pairs={{0,8},{4,36},{8,16},{12,44},{16,24},{20,52},{24,0},{28,60},{32,40}... | collective-permute-start | bytes 2359304 | tf_op jit(solution)/shard_map/ppermute | solution.py:277
  61.2 29.9 %collective-permute-start.17 = (f32[8,192,128]{2,1,0:T(8,128)S(1)}, f32[8,192,128]{2,1,0:T(8,128)S(1)}, u32[]{:S(2)}, u32[]{:S(2)}) collective-permute-start(f32[8,192,128]{2,1,0:T(8,128)S(1)} %get-tuple-element.55), channel_id=1, source_target_pairs={{0,16},{4,68},{8,24},{12,76},{16,0},{20,84},{24,8},{28,92},{32,48}... | collective-permute-start | bytes 2359304 | tf_op jit(solution)/shard_map/ppermute | solution.py:276
  63.9 27.2 %collective-permute-start.18 = (f32[8,192,128]{2,1,0:T(8,128)S(1)}, f32[8,192,128]{2,1,0:T(8,128)S(1)}, u32[]{:S(2)}, u32[]{:S(2)}) collective-permute-start(f32[8,192,128]{2,1,0:T(8,128)S(1)} %get-tuple-element.56), channel_id=1, source_target_pairs={{0,24},{4,100},{8,0},{12,108},{16,8},{20,116},{24,16},{28,124},{32... | collective-permute-start | bytes 2359304 | tf_op jit(solution)/shard_map/ppermute | solution.py:278
  69.0 35.9 %collective-permute-start.6 = (f32[4,200,128]{2,1,0:T(8,128)S(1)}, f32[4,200,128]{2,1,0:T(8,128)S(1)}, u32[]{:S(2)}, u32[]{:S(2)}) collective-permute-start(f32[4,200,128]{2,1,0:T(8,128)S(1)} %get-tuple-element.42), channel_id=1, source_target_pairs={{0,64},{4,20},{8,72},{12,28},{16,80},{20,4},{24,88},{28,12},{32,96... | collective-permute-start | bytes 1228808 | tf_op jit(solution)/shard_map/ppermute | solution.py:285
  72.3 34.2 %collective-permute-start.7 = (f32[4,200,128]{2,1,0:T(8,128)S(1)}, f32[4,200,128]{2,1,0:T(8,128)S(1)}, u32[]{:S(2)}, u32[]{:S(2)}) collective-permute-start(f32[4,200,128]{2,1,0:T(8,128)S(1)} %get-tuple-element.43), channel_id=1, source_target_pairs={{0,32},{4,12},{8,40},{12,20},{16,48},{20,28},{24,56},{28,4},{32,64... | collective-permute-start | bytes 1228808 | tf_op jit(solution)/shard_map/ppermute | solution.py:285
  91.3 9.5 %collective-permute-start.19 = (f32[4,192,128]{2,1,0:T(8,128)S(1)}, f32[4,192,128]{2,1,0:T(8,128)S(1)}, u32[]{:S(2)}, u32[]{:S(2)}) collective-permute-start(f32[4,192,128]{2,1,0:T(8,128)S(1)} %get-tuple-element.57), channel_id=1, source_target_pairs={{0,64},{4,20},{8,72},{12,28},{16,80},{20,4},{24,88},{28,12},{32,96... | collective-permute-start | bytes 1179656 | tf_op jit(solution)/shard_map/ppermute | solution.py:285
  94.3 10.6 %collective-permute-start.20 = (f32[4,192,128]{2,1,0:T(8,128)S(1)}, f32[4,192,128]{2,1,0:T(8,128)S(1)}, u32[]{:S(2)}, u32[]{:S(2)}) collective-permute-start(f32[4,192,128]{2,1,0:T(8,128)S(1)} %get-tuple-element.58), channel_id=1, source_target_pairs={{0,32},{4,12},{8,40},{12,20},{16,48},{20,28},{24,56},{28,4},{32,64... | collective-permute-start | bytes 1179656 | tf_op jit(solution)/shard_map/ppermute | solution.py:285
  94.3 12.3 %collective-permute-start.8 = (f32[4,200,128]{2,1,0:T(8,128)S(1)}, f32[4,200,128]{2,1,0:T(8,128)S(1)}, u32[]{:S(2)}, u32[]{:S(2)}) collective-permute-start(f32[4,200,128]{2,1,0:T(8,128)S(1)} %get-tuple-element.44), channel_id=1, source_target_pairs={{0,96},{4,28},{8,104},{12,4},{16,112},{20,12},{24,120},{28,20},{32... | collective-permute-start | bytes 1228808 | tf_op jit(solution)/shard_map/ppermute | solution.py:285
  100.8 8.9 %collective-permute-start.9 = (f32[4,200,128]{2,1,0:T(8,128)S(1)}, f32[4,200,128]{2,1,0:T(8,128)S(1)}, u32[]{:S(2)}, u32[]{:S(2)}) collective-permute-start(f32[4,200,128]{2,1,0:T(8,128)S(1)} %get-tuple-element.45), channel_id=1, source_target_pairs={{0,68},{4,16},{8,76},{12,24},{16,84},{20,0},{24,92},{28,8},{32,100... | collective-permute-start | bytes 1228808 | tf_op jit(solution)/shard_map/ppermute | solution.py:285
  104.9 9.2 %collective-permute-start.10 = (f32[4,200,128]{2,1,0:T(8,128)S(1)}, f32[4,200,128]{2,1,0:T(8,128)S(1)}, u32[]{:S(2)}, u32[]{:S(2)}) collective-permute-start(f32[4,200,128]{2,1,0:T(8,128)S(1)} %get-tuple-element.46), channel_id=1, source_target_pairs={{0,36},{4,8},{8,44},{12,16},{16,52},{20,24},{24,60},{28,0},{32,68}... | collective-permute-start | bytes 1228808 | tf_op jit(solution)/shard_map/ppermute | solution.py:285
  104.9 10.0 %collective-permute-start.11 = (f32[4,200,128]{2,1,0:T(8,128)S(1)}, f32[4,200,128]{2,1,0:T(8,128)S(1)}, u32[]{:S(2)}, u32[]{:S(2)}) collective-permute-start(f32[4,200,128]{2,1,0:T(8,128)S(1)} %get-tuple-element.47), channel_id=1, source_target_pairs={{0,100},{4,24},{8,108},{12,0},{16,116},{20,8},{24,124},{28,16},{32... | collective-permute-start | bytes 1228808 | tf_op jit(solution)/shard_map/ppermute | solution.py:285
  106.5 10.9 %collective-permute-start.12 = (f32[4,200,128]{2,1,0:T(8,128)S(1)}, f32[4,200,128]{2,1,0:T(8,128)S(1)}, u32[]{:S(2)}, u32[]{:S(2)}) collective-permute-start(f32[4,200,128]{2,1,0:T(8,128)S(1)} %get-tuple-element.48), channel_id=1, source_target_pairs={{0,4},{4,0},{8,12},{12,8},{16,20},{20,16},{24,28},{28,24},{32,36},... | collective-permute-start | bytes 1228808 | tf_op jit(solution)/shard_map/ppermute | solution.py:285
  106.6 13.4 %collective-permute-start.21 = (f32[4,192,128]{2,1,0:T(8,128)S(1)}, f32[4,192,128]{2,1,0:T(8,128)S(1)}, u32[]{:S(2)}, u32[]{:S(2)}) collective-permute-start(f32[4,192,128]{2,1,0:T(8,128)S(1)} %get-tuple-element.59), channel_id=1, source_target_pairs={{0,96},{4,28},{8,104},{12,4},{16,112},{20,12},{24,120},{28,20},{32... | collective-permute-start | bytes 1179656 | tf_op jit(solution)/shard_map/ppermute | solution.py:285
  109.7 10.2 %collective-permute-start.22 = (f32[4,192,128]{2,1,0:T(8,128)S(1)}, f32[4,192,128]{2,1,0:T(8,128)S(1)}, u32[]{:S(2)}, u32[]{:S(2)}) collective-permute-start(f32[4,192,128]{2,1,0:T(8,128)S(1)} %get-tuple-element.60), channel_id=1, source_target_pairs={{0,68},{4,16},{8,76},{12,24},{16,84},{20,0},{24,92},{28,8},{32,100... | collective-permute-start | bytes 1179656 | tf_op jit(solution)/shard_map/ppermute | solution.py:285
  114.1 8.6 %collective-permute-start.23 = (f32[4,192,128]{2,1,0:T(8,128)S(1)}, f32[4,192,128]{2,1,0:T(8,128)S(1)}, u32[]{:S(2)}, u32[]{:S(2)}) collective-permute-start(f32[4,192,128]{2,1,0:T(8,128)S(1)} %get-tuple-element.61), channel_id=1, source_target_pairs={{0,36},{4,8},{8,44},{12,16},{16,52},{20,24},{24,60},{28,0},{32,68}... | collective-permute-start | bytes 1179656 | tf_op jit(solution)/shard_map/ppermute | solution.py:285
  114.9 10.7 %collective-permute-start.24 = (f32[4,192,128]{2,1,0:T(8,128)S(1)}, f32[4,192,128]{2,1,0:T(8,128)S(1)}, u32[]{:S(2)}, u32[]{:S(2)}) collective-permute-start(f32[4,192,128]{2,1,0:T(8,128)S(1)} %get-tuple-element.62), channel_id=1, source_target_pairs={{0,100},{4,24},{8,108},{12,0},{16,116},{20,8},{24,124},{28,16},{32... | collective-permute-start | bytes 1179656 | tf_op jit(solution)/shard_map/ppermute | solution.py:285
  117.4 8.2 %collective-permute-start.25 = (f32[4,192,128]{2,1,0:T(8,128)S(1)}, f32[4,192,128]{2,1,0:T(8,128)S(1)}, u32[]{:S(2)}, u32[]{:S(2)}) collective-permute-start(f32[4,192,128]{2,1,0:T(8,128)S(1)} %get-tuple-element.63), channel_id=1, source_target_pairs={{0,4},{4,0},{8,12},{12,8},{16,20},{20,16},{24,28},{28,24},{32,36},... | collective-permute-start | bytes 1179656 | tf_op jit(solution)/shard_map/ppermute | solution.py:285
where the time goes:
time: 129 us; the launch traced here: 128 us
  waiting for transfers between devices  56.3 us (44%)
  starting transfers between devices  44.2 us (34%)
  Pallas kernels  26.9 us (21%)
    ppermute x14, starting transfers between devices, over_v(): lax.ppermute(parts[q - 1], 'row', second_turn(q // 2, q % 2))  19.9 us
    ppermute x6, waiting for transfers between devices, over_col(): lax.ppermute(bufs[d], 'col', [(z, (z + d) % 4) for z in range(4)])  18.9 us
    ppermute x14, waiting for transfers between devices, over_v(): lax.ppermute(parts[q - 1], 'row', second_turn(q // 2, q % 2))  15.8 us
    pallas_call x1, Pallas kernels, m_packets(): pl.pallas_call(functools.partial(m_kernel, steps), grid=(count, steps), i...  12.9 us
    ppermute x6, starting transfers between devices, over_col(): lax.ppermute(bufs[d], 'col', [(z, (z + d) % 4) for z in range(4)])  11.5 us
    ppermute x2, waiting for transfers between devices, over_u(): two = lax.ppermute(slots[2], 'row', first_turn(2))  11.4 us
    pallas_call x1, Pallas kernels, k_packets(): pl.pallas_call(k_kernel, grid=(count,), in_specs=[SMEM, pl.BlockSpec((1,...  7.1 us
    ppermute x2, waiting for transfers between devices, over_u(): one = lax.ppermute(slots[1], 'row', first_turn(1))  6.76 us
  transfers between devices with their start and end apart: 26, of which 13 were waited for; matrix products, arithmetic and copies ran while one was open for 0% of the time, Pallas kernels for 13%

commit v1 on v0

--- a/solution.py
+++ b/solution.py
@@ -15,13 +15,13 @@
 HEAD = 6 * ROWS
 PKT = HEAD + 8
 STEP = 1024
+SIDE = 8
+HOP = 4
 
 
 F32 = jnp.float32
 VMEM = pl.BlockSpec(memory_space=pltpu.VMEM)
 SMEM = pl.BlockSpec(memory_space=pltpu.SMEM)
-ANY = pl.BlockSpec(memory_space=pl.ANY)
-HBM = pl.BlockSpec(memory_space=pltpu.HBM)
 
 
 def write_packets(s, total, map_ref, outs):
@@ -151,72 +151,104 @@
     return core, u, v
 
 
+def way(code, spot):
+    core, u, v = spot
+    owner = code // (BPO * 16)
+    c = lax.rem(owner, 2)
+    x = lax.rem(owner // 2, 4)
+    y = owner // 8
+    du = lax.rem(jnp.where(core == 0, x, y) - u + 4, 4)
+    dv = lax.rem(jnp.where(core == 0, y, x) - v + 4, 4)
+    return du, dv * 2 + lax.rem(c + core, 2)
+
+
+def slots_of(refs):
+    return [(ref, n) for ref in refs for n in range(ref.shape[0])]
+
+
+def clear(outs):
+    if outs[0].shape[1] == PKT:
+        for out, n in slots_of(outs):
+            out[n, HEAD:PKT, :] = jnp.full((8, 128), -1.0, F32)
+
+
 def pack_kernel(*refs):
-    keys, ins, outs = refs[:4], refs[-8:-4], refs[-4:]
-    core, u, v = place()
-    if outs[0].shape[1] == PKT:
-        empty = jnp.full((8, 128), -1.0, F32)
-        for out in outs:
-            for n in range(8):
-                out[n, HEAD:PKT, :] = empty
-    count = ins[0].shape[0]
-    codes = codes_of([(ref, n) for ref in keys for n in range(count)])
-    for n, code in enumerate(codes):
-        owner = code // (BPO * 16)
-        c = lax.rem(owner, 2)
-        x = lax.rem(owner // 2, 4)
-        y = owner // 8
-        du = lax.rem(jnp.where(core == 0, x, y) - u + 4, 4)
-        dv = lax.rem(jnp.where(core == 0, y, x) - v + 4, 4)
-        slot = dv * 2 + lax.rem(c + core, 2)
-        for k, out in enumerate(outs):
-
-            @pl.when(du == k)
-            def _(out=out, n=n, slot=slot):
-                out[slot] = ins[n // count][n % count]
-
-
-def pack(keys, bufs):
-    bufs = keys if bufs is None else keys + bufs
+    keys, ins, outs = refs[:4], refs[-6:-2], refs[-2:]
+    spot = place()
+    clear(outs)
+    turns = [way(code, spot)[0] for code in codes_of(slots_of(keys))]
+    ones = sum([(du == 1).astype(jnp.int32) for du in turns])
+    twos = sum([(du == 2).astype(jnp.int32) for du in turns])
+    ahead = jnp.minimum(jnp.minimum(HOP, twos), SIDE - ones)
+    used = [jnp.int32(0), jnp.int32(0)]
+    seen = jnp.int32(0)
+    for (ref, n), du in zip(slots_of(ins), turns):
+        far = du == 2
+        early = far & (seen < ahead)
+        seen = seen + far.astype(jnp.int32)
+        for side, goes in enumerate(((du == 1) | early, (du == 3) | (far & ~early))):
+
+            @pl.when(goes)
+            def _(out=outs[side], ref=ref, n=n, slot=used[side]):
+                out[slot] = ref[n]
+
+            used[side] = used[side] + goes.astype(jnp.int32)
+
+
+def hop_kernel(*refs):
+    keys, ins, outs = refs[:2], refs[-4:-2], refs[-2:]
+    spot = place()
+    clear(outs)
+    for key, src, out in zip(keys, ins, outs):
+        used = jnp.int32(0)
+        for (ref, n), code in zip(slots_of([src]), codes_of(slots_of([key]))):
+            goes = (code >= 0) & (way(code, spot)[0] != 0)
+
+            @pl.when(goes)
+            def _(out=out, ref=ref, n=n, slot=used):
+                out[slot] = ref[n]
+
+            used = used + goes.astype(jnp.int32)
+
+
+def turn_kernel(*refs):
+    keys, ins, outs, used = refs[:8], refs[-17:-9], refs[-9:-1], refs[-1]
+    spot = place()
+    clear(outs)
+    for q in range(8):
+        used[q] = 0
+    for (ref, n), code in zip(slots_of(ins), codes_of(slots_of(keys))):
+        du, where = way(code, spot)
+
+        @pl.when((code >= 0) & (du == 0))
+        def _(ref=ref, n=n, where=where):
+            slot = used[where]
+            used[where] = slot + 1
+            for q in range(8):
+
+                @pl.when(where == q)
+                def _(out=outs[q]):
+                    out[slot] = ref[n]
+
+
+def route(kernel, keys, bufs, sizes, scratch=()):
+    ins = list(keys) if bufs is None else list(keys) + list(bufs)
     return pl.pallas_call(
-        pack_kernel,
-        in_specs=[VMEM] * len(bufs),
-        out_specs=[VMEM] * 4,
-        out_shape=[held(8, bufs[-1].shape[1])] * 4,
+        kernel,
+        in_specs=[VMEM] * len(ins),
+        out_specs=[VMEM] * len(sizes),
+        out_shape=[held(n, ins[-1].shape[1]) for n in sizes],
+        scratch_shapes=list(scratch),
         compiler_params=SMALL,
         cost_estimate=pl.CostEstimate(flops=2000000, bytes_accessed=4000000, transcendentals=0),
-        name="pack",
-    )(*near(bufs))
-
-
-def turn_kernel(*refs):
-    ins, outs = refs[:4], refs[4:]
-    for k in range(4):
-        for q in range(1, 8):
-            outs[q - 1][k] = ins[k][q]
-
-
-def turn(bufs):
-    return pl.pallas_call(
-        turn_kernel,
-        in_specs=[VMEM] * 4,
-        out_specs=[VMEM] * 7,
-        out_shape=[held(4, bufs[0].shape[1])] * 7,
-        compiler_params=SMALL,
-        cost_estimate=pl.CostEstimate(flops=2000000, bytes_accessed=6000000, transcendentals=0),
-        name="turn",
-    )(*near(bufs))
+    )(*near(ins))
 
 
 def sum_kernel(*refs):
-    keys, ins, band = refs[:11], refs[-12:-1], refs[-1]
-
-    def slots(some):
-        return [(ref, 0) for ref in some[:4]] + [(ref, n) for ref in some[4:] for n in range(4)]
-
-    codes = codes_of(slots(keys))
+    keys, ins, band = refs[:8], refs[-9:-1], refs[-1]
+    codes = codes_of(slots_of(keys))
     band[...] = jnp.zeros_like(band)
-    for (ref, n), code in zip(slots(ins), codes):
+    for (ref, n), code in zip(slots_of(ins), codes):
 
         @pl.when(code >= 0)
         def _(ref=ref, n=n, code=code):
@@ -267,23 +299,17 @@
 
 def over_col(bufs):
     return [bufs[0]] + [
-        lax.ppermute(bufs[d], "col", [(z, (z + d) % 4) for z in range(4)]) for d in (1, 2, 3)
+        lax.ppermute(bufs[d], "col", [(z, (z + d) % 4) for z in range(4)]) for d in (2, 1, 3)
     ]
 
 
-def over_u(keys, bufs):
-    slots = pack(keys, bufs)
-    two = lax.ppermute(slots[2], "row", first_turn(2))
-    one = lax.ppermute(slots[1], "row", first_turn(1))
-    three = lax.ppermute(slots[3], "row", first_turn(3))
-    return [slots[0], one, two, three]
-
-
-def over_v(slots):
-    parts = turn(slots)
-    return slots + [
-        lax.ppermute(parts[q - 1], "row", second_turn(q // 2, q % 2))
-        for q in (4, 2, 6, 5, 3, 7, 1)
+def beside(bufs, axis):
+    return [lax.ppermute(bufs[0], axis, first_turn(1)), lax.ppermute(bufs[1], axis, first_turn(3))]
+
+
+def over_v(parts):
+    return [parts[0]] + [
+        lax.ppermute(parts[q], "row", second_turn(q // 2, q % 2)) for q in (4, 2, 6, 5, 3, 7, 1)
     ]
 
 
@@ -294,12 +320,26 @@
     k_in = over_col(k_out)
     *m_out, coupling = m_packets(mass_bb, interior_mass, constraint_modes, fixed_modes)
     m_in = over_col(m_out)
-    k_half = over_u(k_in, None)
-    m_half = over_u(k_in, m_in)
-    k_end = over_v(k_half)
-    m_end = over_v(m_half)
-    band_k = assemble(k_end, None)
-    band_m = assemble(k_end, m_end)
+    flow = {"k": {"in": k_in}, "m": {"in": m_in}}
+
+    def stage(kernel, name, took, sizes, scratch=()):
+        for tag in ("k", "m"):
+            keys = [b for t in took for b in flow["k"][t]]
+            bufs = None if tag == "k" else [b for t in took for b in flow[tag][t]]
+            flow[tag][name] = route(kernel, keys, bufs, sizes, scratch)
+
+    def move(name, made, send):
+        for tag in ("k", "m"):
+            flow[tag][name] = send(flow[tag][made])
+
+    stage(pack_kernel, "pack", ("in",), (SIDE, SIDE))
+    move("near", "pack", lambda bufs: beside(bufs, "row"))
+    stage(hop_kernel, "hop", ("near",), (HOP, HOP))
+    move("next", "hop", lambda bufs: beside(bufs, "row"))
+    stage(turn_kernel, "turn", ("in", "near", "next"), (4,) * 8, (pltpu.SMEM((8,), jnp.int32),))
+    move("last", "turn", over_v)
+    band_k = assemble(flow["k"]["last"], None)
+    band_m = assemble(flow["k"]["last"], flow["m"]["last"])
     return band_k, band_m, coupling
 
 

time: 129 us -> 117 us (0.907)
  waiting for transfers between devices: 56.3 us -> 30.9 us
  starting transfers between devices: 44.2 us -> 53.5 us
  Pallas kernels: 26.9 us -> 31.3 us
    ppermute x20 -> x22, waiting for transfers between devices: 37.5 us -> 22.6 us  [the longest x14 12.7 us: over_v(): lax.ppermute(parts[q], 'row', second_turn(q // 2, q % 2))]
    ppermute x6, waiting for transfers between devices: 18.9 us -> 8.31 us  [over_col(): lax.ppermute(bufs[d], 'col', [(z, (z + d) % 4) for z in range(4)])]
    ppermute x20 -> x22, starting transfers between devices: 32.7 us -> 43 us  [the longest x14 29.8 us: over_v(): lax.ppermute(parts[q], 'row', second_turn(q // 2, q % 2))]
    pallas_call x4 -> x6, Pallas kernels: 1.89 us -> 6.3 us  [route(): pl.pallas_call(kernel, in_specs=[VMEM] * len(ins), out_specs=[VMEM] * len...]
  transfers between devices with their start and end apart: 26 -> 28, of which waited for: 13 -> 12; matrix products, arithmetic and copies ran while one was open for 0% -> 0% of each run, Pallas kernels for 13% -> 19%
where the time goes in v1:
time: 117 us; the launch traced here: 116 us
  starting transfers between devices  53.5 us (46%)
  Pallas kernels  31.3 us (27%)
  waiting for transfers between devices  30.9 us (26%)
    ppermute x14, starting transfers between devices, over_v(): lax.ppermute(parts[q], 'row', second_turn(q // 2, q % 2))  29.8 us
    pallas_call x1, Pallas kernels, m_packets(): pl.pallas_call(functools.partial(m_kernel, steps), grid=(count, steps), i...  12.9 us
    ppermute x14, waiting for transfers between devices, over_v(): lax.ppermute(parts[q], 'row', second_turn(q // 2, q % 2))  12.7 us
    ppermute x6, starting transfers between devices, over_col(): lax.ppermute(bufs[d], 'col', [(z, (z + d) % 4) for z in range(4)])  10.5 us
    ppermute x6, waiting for transfers between devices, over_col(): lax.ppermute(bufs[d], 'col', [(z, (z + d) % 4) for z in range(4)])  8.31 us
    ppermute x4, starting transfers between devices, beside(): lax.ppermute(bufs[1], axis, first_turn(3))  8.19 us
    pallas_call x1, Pallas kernels, k_packets(): pl.pallas_call(k_kernel, grid=(count,), in_specs=[SMEM, pl.BlockSpec((1,...  7.1 us
    pallas_call x6, Pallas kernels, route(): pl.pallas_call(kernel, in_specs=[VMEM] * len(ins), out_specs=[VMEM] * len...  6.3 us
  transfers between devices with their start and end apart: 28, of which 12 were waited for; matrix products, arithmetic and copies ran while one was open for 0% of the time, Pallas kernels for 19%

profile of v1, /device:TPU:0, one launch (start us, length us, event | category | flops | bytes accessed | tf_op | source)
XLA Modules:
  0.0 116.5 jit_solution(4752078092735301349)
XLA Ops:
  0.6 7.1 %stiffness.1 = (f32[3,200,128]{2,1,0:T(8,128)S(1)}, f32[3,200,128]{2,1,0:T(8,128)S(1)}, f32[3,200,128]{2,1,0:T(8,128)S(1)}, f32[3,200,128]{2,1,0:T(8,128)S(1)}) custom-call(s32[3,3]{1,0:T(4,128)} %map_ref.1, bf16[3,3,128,384]{3,2,1,0:T(8,128)(2,1)} %bb.2, bf16[3,384,3072]{2,1,0:T(8,128)(2,1)} %bi.1, bf16[3,3072,384]{2,1,0:T(8,128)(2,1)} %cm.3), custom_call_target="tpu_custom_call" | custom-call | flops 1811939328 | bytes 16000000 | tf_op jit(solution)/shard_map/stiffness/pallas_call | solution.py:54
  7.8 4.1 %collective-permute-start = (f32[3,200,128]{2,1,0:T(8,128)S(1)}, f32[3,200,128]{2,1,0:T(8,128)S(1)}, u32[]{:S(2)}, u32[]{:S(2)}) collective-permute-start(f32[3,200,128]{2,1,0:T(8,128)S(1)} %get-tuple-element.37), channel_id=1, source_target_pairs={{0,2},{1,3},{2,0},{3,1},{4,6},{5,7},{6,4},{7,5},{8,10},{9,11},{10,... | collective-permute-start | bytes 921608 | tf_op jit(solution)/shard_map/ppermute | solution.py:302
  11.8 1.0 collective-permute-start.1
  12.8 2.2 %collective-permute-start.2 = (f32[3,200,128]{2,1,0:T(8,128)S(1)}, f32[3,200,128]{2,1,0:T(8,128)S(1)}, u32[]{:S(2)}, u32[]{:S(2)}) collective-permute-start(f32[3,200,128]{2,1,0:T(8,128)S(1)} %get-tuple-element.39), channel_id=1, source_target_pairs={{0,3},{1,0},{2,1},{3,2},{4,7},{5,4},{6,5},{7,6},{8,11},{9,8},{10,9... | collective-permute-start | bytes 921608 | tf_op jit(solution)/shard_map/ppermute | solution.py:302
  15.1 12.9 %mass.1 = (f32[3,192,128]{2,1,0:T(8,128)S(1)}, f32[3,192,128]{2,1,0:T(8,128)S(1)}, f32[3,192,128]{2,1,0:T(8,128)S(1)}, f32[3,192,128]{2,1,0:T(8,128)S(1)}, f32[3,256,384]{2,1,0:T(8,128)}) custom-call(bf16[3,3,128,384]{3,2,1,0:T(8,128)(2,1)} %bb.3, f32[3,3072]{1,0:T(4,128)S(1)} %copy-done, bf16[3,3072,384]{2,1,0:T(8,128)(2,1)} %cm.3, bf16[3,3072,256]{2,1,0:T(8,128)(2,1)} %fm.1), custom_call_target="tpu_custom_call" | custom-call | flops 3623878656 | bytes 14000000 | tf_op jit(solution)/shard_map/mass/pallas_call | solution.py:108
  27.9 0.0 collective-permute-start.14
  27.9 0.9 collective-permute-start.15
  28.8 0.0 collective-permute-done.refs_1_
  28.8 2.4 %collective-permute-start.16 = (f32[3,192,128]{2,1,0:T(8,128)S(1)}, f32[3,192,128]{2,1,0:T(8,128)S(1)}, u32[]{:S(2)}, u32[]{:S(2)}) collective-permute-start(f32[3,192,128]{2,1,0:T(8,128)S(1)} %get-tuple-element.55), channel_id=1, source_target_pairs={{0,3},{1,0},{2,1},{3,2},{4,7},{5,4},{6,5},{7,6},{8,11},{9,8},{10,9... | collective-permute-start | bytes 884744 | tf_op jit(solution)/shard_map/ppermute | solution.py:302
  31.2 0.0 collective-permute-done.1.refs_2_
  31.2 0.0 collective-permute-done.2.refs_3_
  31.2 0.6 shard_map.94
  31.8 1.6 %collective-permute-start.3 = (f32[8,200,128]{2,1,0:T(8,128)S(1)}, f32[8,200,128]{2,1,0:T(8,128)S(1)}, u32[]{:S(2)}, u32[]{:S(2)}) collective-permute-start(f32[8,200,128]{2,1,0:T(8,128)S(1)} %get-tuple-element.40), channel_id=1, source_target_pairs={{0,8},{4,36},{8,16},{12,44},{16,24},{20,52},{24,0},{28,60},{32,40}... | collective-permute-start | bytes 2457608 | tf_op jit(solution)/shard_map/ppermute | solution.py:307
  33.3 1.7 %collective-permute-start.4 = (f32[8,200,128]{2,1,0:T(8,128)S(1)}, f32[8,200,128]{2,1,0:T(8,128)S(1)}, u32[]{:S(2)}, u32[]{:S(2)}) collective-permute-start(f32[8,200,128]{2,1,0:T(8,128)S(1)} %get-tuple-element.41), channel_id=1, source_target_pairs={{0,24},{4,100},{8,0},{12,108},{16,8},{20,116},{24,16},{28,124},{32... | collective-permute-start | bytes 2457608 | tf_op jit(solution)/shard_map/ppermute | solution.py:307
  35.1 4.2 %collective-permute-done.14.refs_5_.refs_9_ = f32[3,192,128]{2,1,0:T(8,128)S(1)} collective-permute-done((f32[3,192,128]{2,1,0:T(8,128)S(1)}, f32[3,192,128]{2,1,0:T(8,128)S(1)}, u32[]{:S(2)}, u32[]{:S(2)}) %collective-permute-start.14) | collective-permute-done | bytes 294944 | tf_op jit(solution)/shard_map/ppermute | solution.py:302
  39.3 4.1 %collective-permute-done.15.refs_6_.refs_10_ = f32[3,192,128]{2,1,0:T(8,128)S(1)} collective-permute-done((f32[3,192,128]{2,1,0:T(8,128)S(1)}, f32[3,192,128]{2,1,0:T(8,128)S(1)}, u32[]{:S(2)}, u32[]{:S(2)}) %collective-permute-start.15) | collective-permute-done | bytes 294944 | tf_op jit(solution)/shard_map/ppermute | solution.py:302
  43.4 0.0 collective-permute-done.16.refs_7_.refs_11_
  43.4 0.6 shard_map.97
  44.0 1.6 %collective-permute-start.17 = (f32[8,192,128]{2,1,0:T(8,128)S(1)}, f32[8,192,128]{2,1,0:T(8,128)S(1)}, u32[]{:S(2)}, u32[]{:S(2)}) collective-permute-start(f32[8,192,128]{2,1,0:T(8,128)S(1)} %get-tuple-element.56), channel_id=1, source_target_pairs={{0,8},{4,36},{8,16},{12,44},{16,24},{20,52},{24,0},{28,60},{32,40}... | collective-permute-start | bytes 2359304 | tf_op jit(solution)/shard_map/ppermute | solution.py:307
  45.5 1.7 %collective-permute-start.18 = (f32[8,192,128]{2,1,0:T(8,128)S(1)}, f32[8,192,128]{2,1,0:T(8,128)S(1)}, u32[]{:S(2)}, u32[]{:S(2)}) collective-permute-start(f32[8,192,128]{2,1,0:T(8,128)S(1)} %get-tuple-element.57), channel_id=1, source_target_pairs={{0,24},{4,100},{8,0},{12,108},{16,8},{20,116},{24,16},{28,124},{32... | collective-permute-start | bytes 2359304 | tf_op jit(solution)/shard_map/ppermute | solution.py:307
  47.3 0.0 collective-permute-done.3.refs_0_.refs_4_
  47.3 0.0 collective-permute-done.4.refs_1_.refs_5_
  47.3 0.7 shard_map.95
  48.0 0.4 collective-permute-start.5
  48.4 3.0 %collective-permute-start.6 = (f32[4,200,128]{2,1,0:T(8,128)S(1)}, f32[4,200,128]{2,1,0:T(8,128)S(1)}, u32[]{:S(2)}, u32[]{:S(2)}) collective-permute-start(f32[4,200,128]{2,1,0:T(8,128)S(1)} %get-tuple-element.43), channel_id=1, source_target_pairs={{0,24},{4,100},{8,0},{12,108},{16,8},{20,116},{24,16},{28,124},{32... | collective-permute-start | bytes 1228808 | tf_op jit(solution)/shard_map/ppermute | solution.py:307
  51.3 5.9 %collective-permute-done.17.refs_2_.refs_12_ = f32[8,192,128]{2,1,0:T(8,128)S(1)} collective-permute-done((f32[8,192,128]{2,1,0:T(8,128)S(1)}, f32[8,192,128]{2,1,0:T(8,128)S(1)}, u32[]{:S(2)}, u32[]{:S(2)}) %collective-permute-start.17) | collective-permute-done | bytes 786464 | tf_op jit(solution)/shard_map/ppermute | solution.py:307
  57.2 0.3 collective-permute-done.18.refs_3_.refs_13_
  57.5 0.7 shard_map.98
  58.3 1.6 %collective-permute-start.19 = (f32[4,192,128]{2,1,0:T(8,128)S(1)}, f32[4,192,128]{2,1,0:T(8,128)S(1)}, u32[]{:S(2)}, u32[]{:S(2)}) collective-permute-start(f32[4,192,128]{2,1,0:T(8,128)S(1)} %get-tuple-element.58), channel_id=1, source_target_pairs={{0,8},{4,36},{8,16},{12,44},{16,24},{20,52},{24,0},{28,60},{32,40}... | collective-permute-start | bytes 1179656 | tf_op jit(solution)/shard_map/ppermute | solution.py:307
  59.8 1.7 %collective-permute-start.20 = (f32[4,192,128]{2,1,0:T(8,128)S(1)}, f32[4,192,128]{2,1,0:T(8,128)S(1)}, u32[]{:S(2)}, u32[]{:S(2)}) collective-permute-start(f32[4,192,128]{2,1,0:T(8,128)S(1)} %get-tuple-element.59), channel_id=1, source_target_pairs={{0,24},{4,100},{8,0},{12,108},{16,8},{20,116},{24,16},{28,124},{32... | collective-permute-start | bytes 1179656 | tf_op jit(solution)/shard_map/ppermute | solution.py:307
  61.6 0.1 collective-permute-done.5.refs_6_
  61.6 0.3 collective-permute-done.6.refs_7_
  61.9 1.9 %shard_map.96 = (f32[4,200,128]{2,1,0:T(8,128)S(1)}, f32[4,200,128]{2,1,0:T(8,128)S(1)}, f32[4,200,128]{2,1,0:T(8,128)S(1)}, f32[4,200,128]{2,1,0:T(8,128)S(1)},...) custom-call(f32[3,200,128]{2,1,0:T(8,128)S(1)} %get-tuple-element.36, ...), custom_call_target="tpu_custom_call" | custom-call | flops 2000000 | bytes 4000000 | tf_op jit(solution)/shard_map/pallas_call | solution.py:236
  63.9 3.3 %collective-permute-start.7 = (f32[4,200,128]{2,1,0:T(8,128)S(1)}, f32[4,200,128]{2,1,0:T(8,128)S(1)}, u32[]{:S(2)}, u32[]{:S(2)}) collective-permute-start(f32[4,200,128]{2,1,0:T(8,128)S(1)} %get-tuple-element.45), channel_id=1, source_target_pairs={{0,64},{4,20},{8,72},{12,28},{16,80},{20,4},{24,88},{28,12},{32,96... | collective-permute-start | bytes 1228808 | tf_op jit(solution)/shard_map/ppermute | solution.py:312
  67.2 0.7 collective-permute-start.8
  67.9 0.0 collective-permute-done.19.refs_14_
  67.9 3.4 %collective-permute-done.20.refs_15_ = f32[4,192,128]{2,1,0:T(8,128)S(1)} collective-permute-done((f32[4,192,128]{2,1,0:T(8,128)S(1)}, f32[4,192,128]{2,1,0:T(8,128)S(1)}, u32[]{:S(2)}, u32[]{:S(2)}) %collective-permute-start.20) | collective-permute-done | bytes 393248 | tf_op jit(solution)/shard_map/ppermute | solution.py:307
  71.3 1.8 %shard_map.99 = (f32[4,192,128]{2,1,0:T(8,128)S(1)}, f32[4,192,128]{2,1,0:T(8,128)S(1)}, f32[4,192,128]{2,1,0:T(8,128)S(1)}, f32[4,192,128]{2,1,0:T(8,128)S(1)},...) custom-call(f32[3,200,128]{2,1,0:T(8,128)S(1)} %get-tuple-element.36, ...), custom_call_target="tpu_custom_call" | custom-call | flops 2000000 | bytes 4000000 | tf_op jit(solution)/shard_map/pallas_call | solution.py:236
  73.0 3.3 %collective-permute-start.21 = (f32[4,192,128]{2,1,0:T(8,128)S(1)}, f32[4,192,128]{2,1,0:T(8,128)S(1)}, u32[]{:S(2)}, u32[]{:S(2)}) collective-permute-start(f32[4,192,128]{2,1,0:T(8,128)S(1)} %get-tuple-element.61), channel_id=1, source_target_pairs={{0,64},{4,20},{8,72},{12,28},{16,80},{20,4},{24,88},{28,12},{32,96... | collective-permute-start | bytes 1179656 | tf_op jit(solution)/shard_map/ppermute | solution.py:312
  76.4 4.9 %collective-permute-start.22 = (f32[4,192,128]{2,1,0:T(8,128)S(1)}, f32[4,192,128]{2,1,0:T(8,128)S(1)}, u32[]{:S(2)}, u32[]{:S(2)}) collective-permute-start(f32[4,192,128]{2,1,0:T(8,128)S(1)} %get-tuple-element.62), channel_id=1, source_target_pairs={{0,32},{4,12},{8,40},{12,20},{16,48},{20,28},{24,56},{28,4},{32,64... | collective-permute-start | bytes 1179656 | tf_op jit(solution)/shard_map/ppermute | solution.py:312
  81.3 0.0 collective-permute-start.9
  81.3 1.1 collective-permute-done.21.refs_9_
  82.4 1.8 %collective-permute-start.10 = (f32[4,200,128]{2,1,0:T(8,128)S(1)}, f32[4,200,128]{2,1,0:T(8,128)S(1)}, u32[]{:S(2)}, u32[]{:S(2)}) collective-permute-start(f32[4,200,128]{2,1,0:T(8,128)S(1)} %get-tuple-element.48), channel_id=1, source_target_pairs={{0,68},{4,16},{8,76},{12,24},{16,84},{20,0},{24,92},{28,8},{32,100... | collective-permute-start | bytes 1228808 | tf_op jit(solution)/shard_map/ppermute | solution.py:312
  84.2 2.4 %collective-permute-done.22.refs_10_ = f32[4,192,128]{2,1,0:T(8,128)S(1)} collective-permute-done((f32[4,192,128]{2,1,0:T(8,128)S(1)}, f32[4,192,128]{2,1,0:T(8,128)S(1)}, u32[]{:S(2)}, u32[]{:S(2)}) %collective-permute-start.22) | collective-permute-done | bytes 393248 | tf_op jit(solution)/shard_map/ppermute | solution.py:312
  86.6 0.0 collective-permute-start.11
  86.6 0.0 collective-permute-done.7.refs_1_
  86.6 1.5 %collective-permute-start.12 = (f32[4,200,128]{2,1,0:T(8,128)S(1)}, f32[4,200,128]{2,1,0:T(8,128)S(1)}, u32[]{:S(2)}, u32[]{:S(2)}) collective-permute-start(f32[4,200,128]{2,1,0:T(8,128)S(1)} %get-tuple-element.50), channel_id=1, source_target_pairs={{0,100},{4,24},{8,108},{12,0},{16,116},{20,8},{24,124},{28,16},{32... | collective-permute-start | bytes 1228808 | tf_op jit(solution)/shard_map/ppermute | solution.py:312
  88.2 0.0 collective-permute-done.8.refs_2_
  88.2 6.7 %collective-permute-start.13 = (f32[4,200,128]{2,1,0:T(8,128)S(1)}, f32[4,200,128]{2,1,0:T(8,128)S(1)}, u32[]{:S(2)}, u32[]{:S(2)}) collective-permute-start(f32[4,200,128]{2,1,0:T(8,128)S(1)} %get-tuple-element.51), channel_id=1, source_target_pairs={{0,4},{4,0},{8,12},{12,8},{16,20},{20,16},{24,28},{28,24},{32,36},... | collective-permute-start | bytes 1228808 | tf_op jit(solution)/shard_map/ppermute | solution.py:312
  94.9 0.0 collective-permute-done.9.refs_3_
  94.9 0.6 collective-permute-start.23
  95.5 0.0 collective-permute-done.10.refs_4_
  95.5 1.8 %collective-permute-start.24 = (f32[4,192,128]{2,1,0:T(8,128)S(1)}, f32[4,192,128]{2,1,0:T(8,128)S(1)}, u32[]{:S(2)}, u32[]{:S(2)}) collective-permute-start(f32[4,192,128]{2,1,0:T(8,128)S(1)} %get-tuple-element.64), channel_id=1, source_target_pairs={{0,68},{4,16},{8,76},{12,24},{16,84},{20,0},{24,92},{28,8},{32,100... | collective-permute-start | bytes 1179656 | tf_op jit(solution)/shard_map/ppermute | solution.py:312
  97.2 0.0 collective-permute-done.11.refs_5_
  97.2 1.1 collective-permute-start.25
  98.4 2.9 %collective-permute-done.12.refs_6_ = f32[4,200,128]{2,1,0:T(8,128)S(1)} collective-permute-done((f32[4,200,128]{2,1,0:T(8,128)S(1)}, f32[4,200,128]{2,1,0:T(8,128)S(1)}, u32[]{:S(2)}, u32[]{:S(2)}) %collective-permute-start.12) | collective-permute-done | bytes 409632 | tf_op jit(solution)/shard_map/ppermute | solution.py:312
  101.3 1.8 %collective-permute-start.26 = (f32[4,192,128]{2,1,0:T(8,128)S(1)}, f32[4,192,128]{2,1,0:T(8,128)S(1)}, u32[]{:S(2)}, u32[]{:S(2)}) collective-permute-start(f32[4,192,128]{2,1,0:T(8,128)S(1)} %get-tuple-element.66), channel_id=1, source_target_pairs={{0,100},{4,24},{8,108},{12,0},{16,116},{20,8},{24,124},{28,16},{32... | collective-permute-start | bytes 1179656 | tf_op jit(solution)/shard_map/ppermute | solution.py:312
  103.1 2.1 %collective-permute-start.27 = (f32[4,192,128]{2,1,0:T(8,128)S(1)}, f32[4,192,128]{2,1,0:T(8,128)S(1)}, u32[]{:S(2)}, u32[]{:S(2)}) collective-permute-start(f32[4,192,128]{2,1,0:T(8,128)S(1)} %get-tuple-element.67), channel_id=1, source_target_pairs={{0,4},{4,0},{8,12},{12,8},{16,20},{20,16},{24,28},{28,24},{32,36},... | collective-permute-start | bytes 1179656 | tf_op jit(solution)/shard_map/ppermute | solution.py:312
  105.1 2.5 %assemble.2 = f32[24,4,32,128]{3,2,1,0:T(8,128)} custom-call(f32[4,200,128]{2,1,0:T(8,128)S(1)} %get-tuple-element.44.refs_0_, f32[4,200,128]{2,1,0:T(8,128)S(1)} %collective-permute-done.7.refs_1_, f32[4,200,128]{2,1,0:T(8,128)S(1)} %collective-permute-done.8.refs_2_, f32[4,200,128]{2,1,0:T(8,128)S(1)} %collective-permute-done.9.refs_3_, ...), custom_call_target="tpu_custom_call" | custom-call | flops 4000000 | bytes 6000000 | tf_op jit(solution)/shard_map/assemble/pallas_call | solution.py:267
  107.7 0.0 collective-permute-done.23.refs_11_
  107.7 0.0 collective-permute-done.24.refs_12_
  107.7 2.4 %collective-permute-done.25.refs_13_ = f32[4,192,128]{2,1,0:T(8,128)S(1)} collective-permute-done((f32[4,192,128]{2,1,0:T(8,128)S(1)}, f32[4,192,128]{2,1,0:T(8,128)S(1)}, u32[]{:S(2)}, u32[]{:S(2)}) %collective-permute-start.25) | collective-permute-done | bytes 393248 | tf_op jit(solution)/shard_map/ppermute | solution.py:312
  110.0 3.9 %collective-permute-done.26.refs_14_ = f32[4,192,128]{2,1,0:T(8,128)S(1)} collective-permute-done((f32[4,192,128]{2,1,0:T(8,128)S(1)}, f32[4,192,128]{2,1,0:T(8,128)S(1)}, u32[]{:S(2)}, u32[]{:S(2)}) %collective-permute-start.26) | collective-permute-done | bytes 393248 | tf_op jit(solution)/shard_map/ppermute | solution.py:312
  113.9 2.5 %assemble.3 = f32[24,4,32,128]{3,2,1,0:T(8,128)} custom-call(f32[4,200,128]{2,1,0:T(8,128)S(1)} %get-tuple-element.44.refs_0_, f32[4,200,128]{2,1,0:T(8,128)S(1)} %collective-permute-done.7.refs_1_, f32[4,200,128]{2,1,0:T(8,128)S(1)} %collective-permute-done.8.refs_2_, f32[4,200,128]{2,1,0:T(8,128)S(1)} %collective-permute-done.9.refs_3_, ...), custom_call_target="tpu_custom_call" | custom-call | flops 4000000 | bytes 6000000 | tf_op jit(solution)/shard_map/assemble/pallas_call | solution.py:267
  (4 shorter events, 0.0 us)
Async XLA Ops:
  0.6 14.4 %copy-start = (f32[3,3072]{1,0:T(4,128)S(1)}, f32[3,3072]{1,0:T(4,128)}, u32[]{:S(2)}) copy-start(f32[3,3072]{1,0:T(4,128)} %im.1) | copy-start | bytes 110596
  7.8 21.1 %collective-permute-start = (f32[3,200,128]{2,1,0:T(8,128)S(1)}, f32[3,200,128]{2,1,0:T(8,128)S(1)}, u32[]{:S(2)}, u32[]{:S(2)}) collective-permute-start(f32[3,200,128]{2,1,0:T(8,128)S(1)} %get-tuple-element.37), channel_id=1, source_target_pairs={{0,2},{1,3},{2,0},{3,1},{4,6},{5,7},{6,4},{7,5},{8,10},{9,11},{10,... | collective-permute-start | bytes 921608 | tf_op jit(solution)/shard_map/ppermute | solution.py:302
  11.8 19.4 %collective-permute-start.1 = (f32[3,200,128]{2,1,0:T(8,128)S(1)}, f32[3,200,128]{2,1,0:T(8,128)S(1)}, u32[]{:S(2)}, u32[]{:S(2)}) collective-permute-start(f32[3,200,128]{2,1,0:T(8,128)S(1)} %get-tuple-element.38), channel_id=1, source_target_pairs={{0,1},{1,2},{2,3},{3,0},{4,5},{5,6},{6,7},{7,4},{8,9},{9,10},{10,1... | collective-permute-start | bytes 921608 | tf_op jit(solution)/shard_map/ppermute | solution.py:302
  12.8 18.3 %collective-permute-start.2 = (f32[3,200,128]{2,1,0:T(8,128)S(1)}, f32[3,200,128]{2,1,0:T(8,128)S(1)}, u32[]{:S(2)}, u32[]{:S(2)}) collective-permute-start(f32[3,200,128]{2,1,0:T(8,128)S(1)} %get-tuple-element.39), channel_id=1, source_target_pairs={{0,3},{1,0},{2,1},{3,2},{4,7},{5,4},{6,5},{7,6},{8,11},{9,8},{10,9... | collective-permute-start | bytes 921608 | tf_op jit(solution)/shard_map/ppermute | solution.py:302
  27.9 11.4 %collective-permute-start.14 = (f32[3,192,128]{2,1,0:T(8,128)S(1)}, f32[3,192,128]{2,1,0:T(8,128)S(1)}, u32[]{:S(2)}, u32[]{:S(2)}) collective-permute-start(f32[3,192,128]{2,1,0:T(8,128)S(1)} %get-tuple-element.53), channel_id=1, source_target_pairs={{0,2},{1,3},{2,0},{3,1},{4,6},{5,7},{6,4},{7,5},{8,10},{9,11},{10,... | collective-permute-start | bytes 884744 | tf_op jit(solution)/shard_map/ppermute | solution.py:302
  27.9 15.4 %collective-permute-start.15 = (f32[3,192,128]{2,1,0:T(8,128)S(1)}, f32[3,192,128]{2,1,0:T(8,128)S(1)}, u32[]{:S(2)}, u32[]{:S(2)}) collective-permute-start(f32[3,192,128]{2,1,0:T(8,128)S(1)} %get-tuple-element.54), channel_id=1, source_target_pairs={{0,1},{1,2},{2,3},{3,0},{4,5},{5,6},{6,7},{7,4},{8,9},{9,10},{10,1... | collective-permute-start | bytes 884744 | tf_op jit(solution)/shard_map/ppermute | solution.py:302
  28.8 14.6 %collective-permute-start.16 = (f32[3,192,128]{2,1,0:T(8,128)S(1)}, f32[3,192,128]{2,1,0:T(8,128)S(1)}, u32[]{:S(2)}, u32[]{:S(2)}) collective-permute-start(f32[3,192,128]{2,1,0:T(8,128)S(1)} %get-tuple-element.55), channel_id=1, source_target_pairs={{0,3},{1,0},{2,1},{3,2},{4,7},{5,4},{6,5},{7,6},{8,11},{9,8},{10,9... | collective-permute-start | bytes 884744 | tf_op jit(solution)/shard_map/ppermute | solution.py:302
  31.8 15.5 %collective-permute-start.3 = (f32[8,200,128]{2,1,0:T(8,128)S(1)}, f32[8,200,128]{2,1,0:T(8,128)S(1)}, u32[]{:S(2)}, u32[]{:S(2)}) collective-permute-start(f32[8,200,128]{2,1,0:T(8,128)S(1)} %get-tuple-element.40), channel_id=1, source_target_pairs={{0,8},{4,36},{8,16},{12,44},{16,24},{20,52},{24,0},{28,60},{32,40}... | collective-permute-start | bytes 2457608 | tf_op jit(solution)/shard_map/ppermute | solution.py:307
  33.3 13.9 %collective-permute-start.4 = (f32[8,200,128]{2,1,0:T(8,128)S(1)}, f32[8,200,128]{2,1,0:T(8,128)S(1)}, u32[]{:S(2)}, u32[]{:S(2)}) collective-permute-start(f32[8,200,128]{2,1,0:T(8,128)S(1)} %get-tuple-element.41), channel_id=1, source_target_pairs={{0,24},{4,100},{8,0},{12,108},{16,8},{20,116},{24,16},{28,124},{32... | collective-permute-start | bytes 2457608 | tf_op jit(solution)/shard_map/ppermute | solution.py:307
  44.0 13.3 %collective-permute-start.17 = (f32[8,192,128]{2,1,0:T(8,128)S(1)}, f32[8,192,128]{2,1,0:T(8,128)S(1)}, u32[]{:S(2)}, u32[]{:S(2)}) collective-permute-start(f32[8,192,128]{2,1,0:T(8,128)S(1)} %get-tuple-element.56), channel_id=1, source_target_pairs={{0,8},{4,36},{8,16},{12,44},{16,24},{20,52},{24,0},{28,60},{32,40}... | collective-permute-start | bytes 2359304 | tf_op jit(solution)/shard_map/ppermute | solution.py:307
  45.5 12.0 %collective-permute-start.18 = (f32[8,192,128]{2,1,0:T(8,128)S(1)}, f32[8,192,128]{2,1,0:T(8,128)S(1)}, u32[]{:S(2)}, u32[]{:S(2)}) collective-permute-start(f32[8,192,128]{2,1,0:T(8,128)S(1)} %get-tuple-element.57), channel_id=1, source_target_pairs={{0,24},{4,100},{8,0},{12,108},{16,8},{20,116},{24,16},{28,124},{32... | collective-permute-start | bytes 2359304 | tf_op jit(solution)/shard_map/ppermute | solution.py:307
  48.0 13.6 %collective-permute-start.5 = (f32[4,200,128]{2,1,0:T(8,128)S(1)}, f32[4,200,128]{2,1,0:T(8,128)S(1)}, u32[]{:S(2)}, u32[]{:S(2)}) collective-permute-start(f32[4,200,128]{2,1,0:T(8,128)S(1)} %get-tuple-element.42), channel_id=1, source_target_pairs={{0,8},{4,36},{8,16},{12,44},{16,24},{20,52},{24,0},{28,60},{32,40}... | collective-permute-start | bytes 1228808 | tf_op jit(solution)/shard_map/ppermute | solution.py:307
  48.4 13.5 %collective-permute-start.6 = (f32[4,200,128]{2,1,0:T(8,128)S(1)}, f32[4,200,128]{2,1,0:T(8,128)S(1)}, u32[]{:S(2)}, u32[]{:S(2)}) collective-permute-start(f32[4,200,128]{2,1,0:T(8,128)S(1)} %get-tuple-element.43), channel_id=1, source_target_pairs={{0,24},{4,100},{8,0},{12,108},{16,8},{20,116},{24,16},{28,124},{32... | collective-permute-start | bytes 1228808 | tf_op jit(solution)/shard_map/ppermute | solution.py:307
  58.3 9.7 %collective-permute-start.19 = (f32[4,192,128]{2,1,0:T(8,128)S(1)}, f32[4,192,128]{2,1,0:T(8,128)S(1)}, u32[]{:S(2)}, u32[]{:S(2)}) collective-permute-start(f32[4,192,128]{2,1,0:T(8,128)S(1)} %get-tuple-element.58), channel_id=1, source_target_pairs={{0,8},{4,36},{8,16},{12,44},{16,24},{20,52},{24,0},{28,60},{32,40}... | collective-permute-start | bytes 1179656 | tf_op jit(solution)/shard_map/ppermute | solution.py:307
  59.8 11.5 %collective-permute-start.20 = (f32[4,192,128]{2,1,0:T(8,128)S(1)}, f32[4,192,128]{2,1,0:T(8,128)S(1)}, u32[]{:S(2)}, u32[]{:S(2)}) collective-permute-start(f32[4,192,128]{2,1,0:T(8,128)S(1)} %get-tuple-element.59), channel_id=1, source_target_pairs={{0,24},{4,100},{8,0},{12,108},{16,8},{20,116},{24,16},{28,124},{32... | collective-permute-start | bytes 1179656 | tf_op jit(solution)/shard_map/ppermute | solution.py:307
  63.9 22.8 %collective-permute-start.7 = (f32[4,200,128]{2,1,0:T(8,128)S(1)}, f32[4,200,128]{2,1,0:T(8,128)S(1)}, u32[]{:S(2)}, u32[]{:S(2)}) collective-permute-start(f32[4,200,128]{2,1,0:T(8,128)S(1)} %get-tuple-element.45), channel_id=1, source_target_pairs={{0,64},{4,20},{8,72},{12,28},{16,80},{20,4},{24,88},{28,12},{32,96... | collective-permute-start | bytes 1228808 | tf_op jit(solution)/shard_map/ppermute | solution.py:312
  67.2 21.0 %collective-permute-start.8 = (f32[4,200,128]{2,1,0:T(8,128)S(1)}, f32[4,200,128]{2,1,0:T(8,128)S(1)}, u32[]{:S(2)}, u32[]{:S(2)}) collective-permute-start(f32[4,200,128]{2,1,0:T(8,128)S(1)} %get-tuple-element.46), channel_id=1, source_target_pairs={{0,32},{4,12},{8,40},{12,20},{16,48},{20,28},{24,56},{28,4},{32,64... | collective-permute-start | bytes 1228808 | tf_op jit(solution)/shard_map/ppermute | solution.py:312
  73.0 9.4 %collective-permute-start.21 = (f32[4,192,128]{2,1,0:T(8,128)S(1)}, f32[4,192,128]{2,1,0:T(8,128)S(1)}, u32[]{:S(2)}, u32[]{:S(2)}) collective-permute-start(f32[4,192,128]{2,1,0:T(8,128)S(1)} %get-tuple-element.61), channel_id=1, source_target_pairs={{0,64},{4,20},{8,72},{12,28},{16,80},{20,4},{24,88},{28,12},{32,96... | collective-permute-start | bytes 1179656 | tf_op jit(solution)/shard_map/ppermute | solution.py:312
  76.4 10.2 %collective-permute-start.22 = (f32[4,192,128]{2,1,0:T(8,128)S(1)}, f32[4,192,128]{2,1,0:T(8,128)S(1)}, u32[]{:S(2)}, u32[]{:S(2)}) collective-permute-start(f32[4,192,128]{2,1,0:T(8,128)S(1)} %get-tuple-element.62), channel_id=1, source_target_pairs={{0,32},{4,12},{8,40},{12,20},{16,48},{20,28},{24,56},{28,4},{32,64... | collective-permute-start | bytes 1179656 | tf_op jit(solution)/shard_map/ppermute | solution.py:312
  81.3 13.6 %collective-permute-start.9 = (f32[4,200,128]{2,1,0:T(8,128)S(1)}, f32[4,200,128]{2,1,0:T(8,128)S(1)}, u32[]{:S(2)}, u32[]{:S(2)}) collective-permute-start(f32[4,200,128]{2,1,0:T(8,128)S(1)} %get-tuple-element.47), channel_id=1, source_target_pairs={{0,96},{4,28},{8,104},{12,4},{16,112},{20,12},{24,120},{28,20},{32... | collective-permute-start | bytes 1228808 | tf_op jit(solution)/shard_map/ppermute | solution.py:312
  82.4 13.0 %collective-permute-start.10 = (f32[4,200,128]{2,1,0:T(8,128)S(1)}, f32[4,200,128]{2,1,0:T(8,128)S(1)}, u32[]{:S(2)}, u32[]{:S(2)}) collective-permute-start(f32[4,200,128]{2,1,0:T(8,128)S(1)} %get-tuple-element.48), channel_id=1, source_target_pairs={{0,68},{4,16},{8,76},{12,24},{16,84},{20,0},{24,92},{28,8},{32,100... | collective-permute-start | bytes 1228808 | tf_op jit(solution)/shard_map/ppermute | solution.py:312
  86.6 10.6 %collective-permute-start.11 = (f32[4,200,128]{2,1,0:T(8,128)S(1)}, f32[4,200,128]{2,1,0:T(8,128)S(1)}, u32[]{:S(2)}, u32[]{:S(2)}) collective-permute-start(f32[4,200,128]{2,1,0:T(8,128)S(1)} %get-tuple-element.49), channel_id=1, source_target_pairs={{0,36},{4,8},{8,44},{12,16},{16,52},{20,24},{24,60},{28,0},{32,68}... | collective-permute-start | bytes 1228808 | tf_op jit(solution)/shard_map/ppermute | solution.py:312
  86.6 14.6 %collective-permute-start.12 = (f32[4,200,128]{2,1,0:T(8,128)S(1)}, f32[4,200,128]{2,1,0:T(8,128)S(1)}, u32[]{:S(2)}, u32[]{:S(2)}) collective-permute-start(f32[4,200,128]{2,1,0:T(8,128)S(1)} %get-tuple-element.50), channel_id=1, source_target_pairs={{0,100},{4,24},{8,108},{12,0},{16,116},{20,8},{24,124},{28,16},{32... | collective-permute-start | bytes 1228808 | tf_op jit(solution)/shard_map/ppermute | solution.py:312
  88.2 14.9 %collective-permute-start.13 = (f32[4,200,128]{2,1,0:T(8,128)S(1)}, f32[4,200,128]{2,1,0:T(8,128)S(1)}, u32[]{:S(2)}, u32[]{:S(2)}) collective-permute-start(f32[4,200,128]{2,1,0:T(8,128)S(1)} %get-tuple-element.51), channel_id=1, source_target_pairs={{0,4},{4,0},{8,12},{12,8},{16,20},{20,16},{24,28},{28,24},{32,36},... | collective-permute-start | bytes 1228808 | tf_op jit(solution)/shard_map/ppermute | solution.py:312
  94.9 12.8 %collective-permute-start.23 = (f32[4,192,128]{2,1,0:T(8,128)S(1)}, f32[4,192,128]{2,1,0:T(8,128)S(1)}, u32[]{:S(2)}, u32[]{:S(2)}) collective-permute-start(f32[4,192,128]{2,1,0:T(8,128)S(1)} %get-tuple-element.63), channel_id=1, source_target_pairs={{0,96},{4,28},{8,104},{12,4},{16,112},{20,12},{24,120},{28,20},{32... | collective-permute-start | bytes 1179656 | tf_op jit(solution)/shard_map/ppermute | solution.py:312
  95.5 12.2 %collective-permute-start.24 = (f32[4,192,128]{2,1,0:T(8,128)S(1)}, f32[4,192,128]{2,1,0:T(8,128)S(1)}, u32[]{:S(2)}, u32[]{:S(2)}) collective-permute-start(f32[4,192,128]{2,1,0:T(8,128)S(1)} %get-tuple-element.64), channel_id=1, source_target_pairs={{0,68},{4,16},{8,76},{12,24},{16,84},{20,0},{24,92},{28,8},{32,100... | collective-permute-start | bytes 1179656 | tf_op jit(solution)/shard_map/ppermute | solution.py:312
  97.2 12.8 %collective-permute-start.25 = (f32[4,192,128]{2,1,0:T(8,128)S(1)}, f32[4,192,128]{2,1,0:T(8,128)S(1)}, u32[]{:S(2)}, u32[]{:S(2)}) collective-permute-start(f32[4,192,128]{2,1,0:T(8,128)S(1)} %get-tuple-element.65), channel_id=1, source_target_pairs={{0,36},{4,8},{8,44},{12,16},{16,52},{20,24},{24,60},{28,0},{32,68}... | collective-permute-start | bytes 1179656 | tf_op jit(solution)/shard_map/ppermute | solution.py:312
  101.3 12.7 %collective-permute-start.26 = (f32[4,192,128]{2,1,0:T(8,128)S(1)}, f32[4,192,128]{2,1,0:T(8,128)S(1)}, u32[]{:S(2)}, u32[]{:S(2)}) collective-permute-start(f32[4,192,128]{2,1,0:T(8,128)S(1)} %get-tuple-element.66), channel_id=1, source_target_pairs={{0,100},{4,24},{8,108},{12,0},{16,116},{20,8},{24,124},{28,16},{32... | collective-permute-start | bytes 1179656 | tf_op jit(solution)/shard_map/ppermute | solution.py:312
  103.1 10.9 %collective-permute-start.27 = (f32[4,192,128]{2,1,0:T(8,128)S(1)}, f32[4,192,128]{2,1,0:T(8,128)S(1)}, u32[]{:S(2)}, u32[]{:S(2)}) collective-permute-start(f32[4,192,128]{2,1,0:T(8,128)S(1)} %get-tuple-element.67), channel_id=1, source_target_pairs={{0,4},{4,0},{8,12},{12,8},{16,20},{20,16},{24,28},{28,24},{32,36},... | collective-permute-start | bytes 1179656 | tf_op jit(solution)/shard_map/ppermute | solution.py:312

commit v2 on v1

--- a/solution.py
+++ b/solution.py
@@ -1,5 +1,3 @@
-import functools
-
 import jax
 import jax.numpy as jnp
 from jax import lax
@@ -14,7 +12,6 @@
 ROWS = 32
 HEAD = 6 * ROWS
 PKT = HEAD + 8
-STEP = 1024
 SIDE = 8
 HOP = 4
 
@@ -71,59 +68,79 @@
     )(bmap, stiff_bb, stiff_bi, cm)
 
 
-def m_kernel(steps, bb, im, cm, fm, o0, o1, o2, o3, coup, total, w):
-    s, k = pl.program_id(0), pl.program_id(1)
-
-    @pl.when(k == 0)
-    def _():
-        for i in range(3):
-            total[i * 128 : (i + 1) * 128, :] = bb[0, i].astype(F32)
-        coup[...] = jnp.zeros_like(coup)
-
-    for j in range(STEP // 128):
-        lines = im[:, pl.ds(pl.multiple_of(k * STEP + j * 128, 128), 128)]
+def weigh(s, im, cm, w):
+    for j in range(w.shape[0] // 128):
+        part = slice(j * 128, (j + 1) * 128)
+        lines = im[:, part]
         mine = lax.broadcasted_iota(jnp.int32, lines.shape, 0) == s
         line = jnp.sum(jnp.where(mine, lines, 0.0), axis=0, keepdims=True)
         column = jnp.broadcast_to(line, (128, 128)).T
-        part = slice(j * 128, (j + 1) * 128)
-        for i in range(3):
+        for i in range(w.shape[1] // 128):
             lanes = slice(i * 128, (i + 1) * 128)
             w[part, lanes] = (column * cm[0, part, lanes].astype(F32)).astype(jnp.bfloat16)
-    dims = (((0,), (0,)), ((), ()))
-    total[0:128, :] += lax.dot_general(cm[0, :, 0:128], w[...], dims, preferred_element_type=F32)
+
+
+DOWN = (((0,), (0,)), ((), ()))
+
+
+def m_kernel(bb, im, cm, o0, o1, o2, o3, total, w):
+    s = pl.program_id(0)
+    weigh(s, im, cm, w)
+    for i in range(3):
+        total[i * 128 : (i + 1) * 128, :] = bb[0, i].astype(F32)
+    total[0:128, :] += lax.dot_general(cm[0, :, 0:128], w[...], DOWN, preferred_element_type=F32)
     total[128:384, 128:384] += lax.dot_general(
-        cm[0, :, 128:384], w[:, 128:384], dims, preferred_element_type=F32
+        cm[0, :, 128:384], w[:, 128:384], DOWN, preferred_element_type=F32
     )
-    coup[0] += lax.dot_general(fm[0], w[...], dims, preferred_element_type=F32)
-
-    @pl.when(k == steps - 1)
-    def _():
-        write_packets(s, total, None, (o0, o1, o2, o3))
-
-
-def m_packets(mass_bb, im, cm, fm):
+    write_packets(s, total, None, (o0, o1, o2, o3))
+
+
+def m_packets(mass_bb, im, cm):
+    count, inner, order = cm.shape
+    return pl.pallas_call(
+        m_kernel,
+        grid=(count,),
+        in_specs=[
+            pl.BlockSpec((1, 3, 128, order), lambda s: (s, 0, 0, 0)),
+            pl.BlockSpec((count, inner), lambda s: (0, 0)),
+            pl.BlockSpec((1, inner, order), lambda s: (s, 0, 0)),
+        ],
+        out_specs=[VMEM] * 4,
+        out_shape=[held(count, HEAD)] * 4,
+        compiler_params=pltpu.CompilerParams(vmem_limit_bytes=52 << 20),
+        scratch_shapes=[pltpu.VMEM((order, order), F32), pltpu.VMEM((inner, order), jnp.bfloat16)],
+        cost_estimate=pl.CostEstimate(
+            flops=6 * count * 128 * 128 * inner * 2, bytes_accessed=9000000, transcendentals=0
+        ),
+        name="mass",
+    )(mass_bb, im, cm)
+
+
+def c_kernel(im, cm, fm, coup, w):
+    weigh(pl.program_id(0), im, cm, w)
+    coup[0] = lax.dot_general(fm[0], w[...], DOWN, preferred_element_type=F32)
+
+
+def couple(im, cm, fm):
     count, inner, order = cm.shape
     modes = fm.shape[2]
-    steps = inner // STEP
-    return pl.pallas_call(
-        functools.partial(m_kernel, steps),
-        grid=(count, steps),
+    return pl.pallas_call(
+        c_kernel,
+        grid=(count,),
         in_specs=[
-            pl.BlockSpec((1, 3, 128, order), lambda s, k: (s, 0, 0, 0)),
-            pl.BlockSpec((count, inner), lambda s, k: (0, 0)),
-            pl.BlockSpec((1, STEP, order), lambda s, k: (s, k, 0)),
-            pl.BlockSpec((1, STEP, modes), lambda s, k: (s, k, 0)),
+            pl.BlockSpec((count, inner), lambda s: (0, 0)),
+            pl.BlockSpec((1, inner, order), lambda s: (s, 0, 0)),
+            pl.BlockSpec((1, inner, modes), lambda s: (s, 0, 0)),
         ],
-        compiler_params=pltpu.CompilerParams(vmem_limit_bytes=52 << 20),
-        out_specs=[VMEM] * 4
-        + [pl.BlockSpec((1, modes, order), lambda s, k: (s, 0, 0))],
-        out_shape=[held(count, HEAD)] * 4 + [jax.ShapeDtypeStruct((count, modes, order), F32)],
-        scratch_shapes=[pltpu.VMEM((order, order), F32), pltpu.VMEM((STEP, order), jnp.bfloat16)],
+        out_specs=pl.BlockSpec((1, modes, order), lambda s: (s, 0, 0)),
+        out_shape=jax.ShapeDtypeStruct((count, modes, order), F32),
+        compiler_params=pltpu.CompilerParams(vmem_limit_bytes=40 << 20),
+        scratch_shapes=[pltpu.VMEM((inner, order), jnp.bfloat16)],
         cost_estimate=pl.CostEstimate(
-            flops=12 * count * 128 * 128 * inner * 2, bytes_accessed=14000000, transcendentals=0
+            flops=6 * count * 128 * 128 * inner * 2, bytes_accessed=12000000, transcendentals=0
         ),
-        name="mass",
-    )(mass_bb, im, cm, fm)
+        name="couple",
+    )(im, cm, fm)
 
 
 SMALL = pltpu.CompilerParams(vmem_limit_bytes=4 << 20)
@@ -318,7 +335,7 @@
 ):
     k_out = k_packets(boundary_map, stiff_bb, stiff_bi, constraint_modes)
     k_in = over_col(k_out)
-    *m_out, coupling = m_packets(mass_bb, interior_mass, constraint_modes, fixed_modes)
+    m_out = m_packets(mass_bb, interior_mass, constraint_modes)
     m_in = over_col(m_out)
     flow = {"k": {"in": k_in}, "m": {"in": m_in}}
 
@@ -338,6 +355,7 @@
     move("next", "hop", lambda bufs: beside(bufs, "row"))
     stage(turn_kernel, "turn", ("in", "near", "next"), (4,) * 8, (pltpu.SMEM((8,), jnp.int32),))
     move("last", "turn", over_v)
+    coupling = couple(interior_mass, constraint_modes, fixed_modes)
     band_k = assemble(flow["k"]["last"], None)
     band_m = assemble(flow["k"]["last"], flow["m"]["last"])
     return band_k, band_m, coupling

time: 117 us -> 109 us (0.932)
  starting transfers between devices: 53.5 us -> 42.3 us
  waiting for transfers between devices: 30.9 us -> 34.9 us
    ppermute x14, starting transfers between devices: 29.8 us -> 18.3 us  [over_v(): lax.ppermute(parts[q], 'row', second_turn(q // 2, q % 2))]
    ppermute x14, waiting for transfers between devices: 12.7 us -> 18.9 us  [over_v(): lax.ppermute(parts[q], 'row', second_turn(q // 2, q % 2))]
    ppermute x4, waiting for transfers between devices: 3.91 us -> 0.57 us  [beside(): lax.ppermute(bufs[1], axis, first_turn(3))]
    pallas_call x1 -> x2, Pallas kernels: 12.9 us -> 12.3 us  [the longest x1 7.31 us: m_packets(): pl.pallas_call(m_kernel, grid=(count,), in_specs=[pl.BlockSpec((1, 3, 128...]
  transfers between devices with their start and end apart: 28 -> 28, of which waited for: 12 -> 13; matrix products, arithmetic and copies ran while one was open for 0% -> 0% of each run, Pallas kernels for 19% -> 19%
where the time goes in v2:
time: 109 us
  starting transfers between devices  42.3 us (39%)
  waiting for transfers between devices  34.9 us (32%)
  Pallas kernels  30.7 us (28%)
    ppermute x14, waiting for transfers between devices, over_v(): lax.ppermute(parts[q], 'row', second_turn(q // 2, q % 2))  18.9 us
    ppermute x14, starting transfers between devices, over_v(): lax.ppermute(parts[q], 'row', second_turn(q // 2, q % 2))  18.3 us
    ppermute x6, starting transfers between devices, over_col(): lax.ppermute(bufs[d], 'col', [(z, (z + d) % 4) for z in range(4)])  10.7 us
    ppermute x6, waiting for transfers between devices, over_col(): lax.ppermute(bufs[d], 'col', [(z, (z + d) % 4) for z in range(4)])  9.46 us
    ppermute x4, starting transfers between devices, beside(): lax.ppermute(bufs[1], axis, first_turn(3))  7.95 us
    pallas_call x1, Pallas kernels, m_packets(): pl.pallas_call(m_kernel, grid=(count,), in_specs=[pl.BlockSpec((1, 3, 128...  7.31 us
    pallas_call x1, Pallas kernels, k_packets(): pl.pallas_call(k_kernel, grid=(count,), in_specs=[SMEM, pl.BlockSpec((1,...  7.1 us
    pallas_call x6, Pallas kernels, route(): pl.pallas_call(kernel, in_specs=[VMEM] * len(ins), out_specs=[VMEM] * len...  6.3 us
  transfers between devices with their start and end apart: 28, of which 13 were waited for; matrix products, arithmetic and copies ran while one was open for 0% of the time, Pallas kernels for 19%

profile of v2, /device:TPU:0, one launch (start us, length us, event | category | flops | bytes accessed | tf_op | source)
XLA Modules:
  0.0 108.7 jit_solution(4467295104645354253)
XLA Ops:
  0.6 7.1 %stiffness.1 = (f32[3,200,128]{2,1,0:T(8,128)S(1)}, f32[3,200,128]{2,1,0:T(8,128)S(1)}, f32[3,200,128]{2,1,0:T(8,128)S(1)}, f32[3,200,128]{2,1,0:T(8,128)S(1)}) custom-call(s32[3,3]{1,0:T(4,128)} %map_ref.1, bf16[3,3,128,384]{3,2,1,0:T(8,128)(2,1)} %bb.2, bf16[3,384,3072]{2,1,0:T(8,128)(2,1)} %bi.1, bf16[3,3072,384]{2,1,0:T(8,128)(2,1)} %cm.5), custom_call_target="tpu_custom_call" | custom-call | flops 1811939328 | bytes 16000000 | tf_op jit(solution)/shard_map/stiffness/pallas_call | solution.py:51
  7.8 4.1 %collective-permute-start = (f32[3,200,128]{2,1,0:T(8,128)S(1)}, f32[3,200,128]{2,1,0:T(8,128)S(1)}, u32[]{:S(2)}, u32[]{:S(2)}) collective-permute-start(f32[3,200,128]{2,1,0:T(8,128)S(1)} %get-tuple-element.36), channel_id=1, source_target_pairs={{0,2},{1,3},{2,0},{3,1},{4,6},{5,7},{6,4},{7,5},{8,10},{9,11},{10,... | collective-permute-start | bytes 921608 | tf_op jit(solution)/shard_map/ppermute | solution.py:319
  11.8 1.0 collective-permute-start.1
  12.8 2.2 %collective-permute-start.2 = (f32[3,200,128]{2,1,0:T(8,128)S(1)}, f32[3,200,128]{2,1,0:T(8,128)S(1)}, u32[]{:S(2)}, u32[]{:S(2)}) collective-permute-start(f32[3,200,128]{2,1,0:T(8,128)S(1)} %get-tuple-element.38), channel_id=1, source_target_pairs={{0,3},{1,0},{2,1},{3,2},{4,7},{5,4},{6,5},{7,6},{8,11},{9,8},{10,9... | collective-permute-start | bytes 921608 | tf_op jit(solution)/shard_map/ppermute | solution.py:319
  15.1 7.3 %mass.1 = (f32[3,192,128]{2,1,0:T(8,128)S(1)}, f32[3,192,128]{2,1,0:T(8,128)S(1)}, f32[3,192,128]{2,1,0:T(8,128)S(1)}, f32[3,192,128]{2,1,0:T(8,128)S(1)}) custom-call(bf16[3,3,128,384]{3,2,1,0:T(8,128)(2,1)} %bb.3, f32[3,3072]{1,0:T(4,128)S(1)} %copy-done, bf16[3,3072,384]{2,1,0:T(8,128)(2,1)} %cm.5), custom_call_target="tpu_custom_call" | custom-call | flops 1811939328 | bytes 9000000 | tf_op jit(solution)/shard_map/mass/pallas_call | solution.py:100
  22.4 0.1 collective-permute-start.14
  22.5 0.9 collective-permute-start.15
  23.3 0.0 collective-permute-done.refs_1_
  23.4 2.4 %collective-permute-start.16 = (f32[3,192,128]{2,1,0:T(8,128)S(1)}, f32[3,192,128]{2,1,0:T(8,128)S(1)}, u32[]{:S(2)}, u32[]{:S(2)}) collective-permute-start(f32[3,192,128]{2,1,0:T(8,128)S(1)} %get-tuple-element.54), channel_id=1, source_target_pairs={{0,3},{1,0},{2,1},{3,2},{4,7},{5,4},{6,5},{7,6},{8,11},{9,8},{10,9... | collective-permute-start | bytes 884744 | tf_op jit(solution)/shard_map/ppermute | solution.py:319
  25.8 0.3 collective-permute-done.1.refs_2_
  26.1 1.5 %collective-permute-done.2.refs_3_ = f32[3,200,128]{2,1,0:T(8,128)S(1)} collective-permute-done((f32[3,200,128]{2,1,0:T(8,128)S(1)}, f32[3,200,128]{2,1,0:T(8,128)S(1)}, u32[]{:S(2)}, u32[]{:S(2)}) %collective-permute-start.2) | collective-permute-done | bytes 307232 | tf_op jit(solution)/shard_map/ppermute | solution.py:319
  27.6 0.6 shard_map.94
  28.2 1.6 %collective-permute-start.3 = (f32[8,200,128]{2,1,0:T(8,128)S(1)}, f32[8,200,128]{2,1,0:T(8,128)S(1)}, u32[]{:S(2)}, u32[]{:S(2)}) collective-permute-start(f32[8,200,128]{2,1,0:T(8,128)S(1)} %get-tuple-element.39), channel_id=1, source_target_pairs={{0,8},{4,36},{8,16},{12,44},{16,24},{20,52},{24,0},{28,60},{32,40}... | collective-permute-start | bytes 2457608 | tf_op jit(solution)/shard_map/ppermute | solution.py:324
  29.7 1.7 %collective-permute-start.4 = (f32[8,200,128]{2,1,0:T(8,128)S(1)}, f32[8,200,128]{2,1,0:T(8,128)S(1)}, u32[]{:S(2)}, u32[]{:S(2)}) collective-permute-start(f32[8,200,128]{2,1,0:T(8,128)S(1)} %get-tuple-element.40), channel_id=1, source_target_pairs={{0,24},{4,100},{8,0},{12,108},{16,8},{20,116},{24,16},{28,124},{32... | collective-permute-start | bytes 2457608 | tf_op jit(solution)/shard_map/ppermute | solution.py:324
  31.5 2.4 %collective-permute-done.14.refs_5_.refs_9_ = f32[3,192,128]{2,1,0:T(8,128)S(1)} collective-permute-done((f32[3,192,128]{2,1,0:T(8,128)S(1)}, f32[3,192,128]{2,1,0:T(8,128)S(1)}, u32[]{:S(2)}, u32[]{:S(2)}) %collective-permute-start.14) | collective-permute-done | bytes 294944 | tf_op jit(solution)/shard_map/ppermute | solution.py:319
  33.8 4.5 %collective-permute-done.15.refs_6_.refs_10_ = f32[3,192,128]{2,1,0:T(8,128)S(1)} collective-permute-done((f32[3,192,128]{2,1,0:T(8,128)S(1)}, f32[3,192,128]{2,1,0:T(8,128)S(1)}, u32[]{:S(2)}, u32[]{:S(2)}) %collective-permute-start.15) | collective-permute-done | bytes 294944 | tf_op jit(solution)/shard_map/ppermute | solution.py:319
  38.3 0.8 collective-permute-done.16.refs_7_.refs_11_
  39.1 0.6 shard_map.97
  39.7 1.6 %collective-permute-start.17 = (f32[8,192,128]{2,1,0:T(8,128)S(1)}, f32[8,192,128]{2,1,0:T(8,128)S(1)}, u32[]{:S(2)}, u32[]{:S(2)}) collective-permute-start(f32[8,192,128]{2,1,0:T(8,128)S(1)} %get-tuple-element.55), channel_id=1, source_target_pairs={{0,8},{4,36},{8,16},{12,44},{16,24},{20,52},{24,0},{28,60},{32,40}... | collective-permute-start | bytes 2359304 | tf_op jit(solution)/shard_map/ppermute | solution.py:324
  41.3 1.7 %collective-permute-start.18 = (f32[8,192,128]{2,1,0:T(8,128)S(1)}, f32[8,192,128]{2,1,0:T(8,128)S(1)}, u32[]{:S(2)}, u32[]{:S(2)}) collective-permute-start(f32[8,192,128]{2,1,0:T(8,128)S(1)} %get-tuple-element.56), channel_id=1, source_target_pairs={{0,24},{4,100},{8,0},{12,108},{16,8},{20,116},{24,16},{28,124},{32... | collective-permute-start | bytes 2359304 | tf_op jit(solution)/shard_map/ppermute | solution.py:324
  43.0 0.0 collective-permute-done.3.refs_0_.refs_4_
  43.0 0.0 collective-permute-done.4.refs_1_.refs_5_
  43.0 0.0 slice-start.2
  43.1 0.7 shard_map.95
  43.8 0.6 collective-permute-start.5
  44.4 2.7 %collective-permute-start.6 = (f32[4,200,128]{2,1,0:T(8,128)S(1)}, f32[4,200,128]{2,1,0:T(8,128)S(1)}, u32[]{:S(2)}, u32[]{:S(2)}) collective-permute-start(f32[4,200,128]{2,1,0:T(8,128)S(1)} %get-tuple-element.42), channel_id=1, source_target_pairs={{0,24},{4,100},{8,0},{12,108},{16,8},{20,116},{24,16},{28,124},{32... | collective-permute-start | bytes 1228808 | tf_op jit(solution)/shard_map/ppermute | solution.py:324
  47.1 5.9 %collective-permute-done.17.refs_2_.refs_12_ = f32[8,192,128]{2,1,0:T(8,128)S(1)} collective-permute-done((f32[8,192,128]{2,1,0:T(8,128)S(1)}, f32[8,192,128]{2,1,0:T(8,128)S(1)}, u32[]{:S(2)}, u32[]{:S(2)}) %collective-permute-start.17) | collective-permute-done | bytes 786464 | tf_op jit(solution)/shard_map/ppermute | solution.py:324
  53.0 0.3 collective-permute-done.18.refs_3_.refs_13_
  53.3 0.7 shard_map.98
  54.0 1.6 %collective-permute-start.19 = (f32[4,192,128]{2,1,0:T(8,128)S(1)}, f32[4,192,128]{2,1,0:T(8,128)S(1)}, u32[]{:S(2)}, u32[]{:S(2)}) collective-permute-start(f32[4,192,128]{2,1,0:T(8,128)S(1)} %get-tuple-element.57), channel_id=1, source_target_pairs={{0,8},{4,36},{8,16},{12,44},{16,24},{20,52},{24,0},{28,60},{32,40}... | collective-permute-start | bytes 1179656 | tf_op jit(solution)/shard_map/ppermute | solution.py:324
  55.6 1.7 %collective-permute-start.20 = (f32[4,192,128]{2,1,0:T(8,128)S(1)}, f32[4,192,128]{2,1,0:T(8,128)S(1)}, u32[]{:S(2)}, u32[]{:S(2)}) collective-permute-start(f32[4,192,128]{2,1,0:T(8,128)S(1)} %get-tuple-element.58), channel_id=1, source_target_pairs={{0,24},{4,100},{8,0},{12,108},{16,8},{20,116},{24,16},{28,124},{32... | collective-permute-start | bytes 1179656 | tf_op jit(solution)/shard_map/ppermute | solution.py:324
  57.3 0.1 collective-permute-done.5.refs_6_
  57.4 0.3 collective-permute-done.6.refs_7_
  57.7 1.9 %shard_map.96 = (f32[4,200,128]{2,1,0:T(8,128)S(1)}, f32[4,200,128]{2,1,0:T(8,128)S(1)}, f32[4,200,128]{2,1,0:T(8,128)S(1)}, f32[4,200,128]{2,1,0:T(8,128)S(1)},...) custom-call(f32[3,200,128]{2,1,0:T(8,128)S(1)} %get-tuple-element.35, ...), custom_call_target="tpu_custom_call" | custom-call | flops 2000000 | bytes 4000000 | tf_op jit(solution)/shard_map/pallas_call | solution.py:253
  59.6 1.0 collective-permute-start.10
  60.6 3.3 %collective-permute-start.11 = (f32[4,200,128]{2,1,0:T(8,128)S(1)}, f32[4,200,128]{2,1,0:T(8,128)S(1)}, u32[]{:S(2)}, u32[]{:S(2)}) collective-permute-start(f32[4,200,128]{2,1,0:T(8,128)S(1)} %get-tuple-element.48), channel_id=1, source_target_pairs={{0,36},{4,8},{8,44},{12,16},{16,52},{20,24},{24,60},{28,0},{32,68}... | collective-permute-start | bytes 1228808 | tf_op jit(solution)/shard_map/ppermute | solution.py:329
  64.0 0.0 collective-permute-done.19.refs_14_
  64.0 0.0 collective-permute-done.20.refs_15_
  64.0 1.8 %shard_map.99 = (f32[4,192,128]{2,1,0:T(8,128)S(1)}, f32[4,192,128]{2,1,0:T(8,128)S(1)}, f32[4,192,128]{2,1,0:T(8,128)S(1)}, f32[4,192,128]{2,1,0:T(8,128)S(1)},...) custom-call(f32[3,200,128]{2,1,0:T(8,128)S(1)} %get-tuple-element.35, ...), custom_call_target="tpu_custom_call" | custom-call | flops 2000000 | bytes 4000000 | tf_op jit(solution)/shard_map/pallas_call | solution.py:253
  65.7 3.0 %collective-permute-start.21 = (f32[4,192,128]{2,1,0:T(8,128)S(1)}, f32[4,192,128]{2,1,0:T(8,128)S(1)}, u32[]{:S(2)}, u32[]{:S(2)}) collective-permute-start(f32[4,192,128]{2,1,0:T(8,128)S(1)} %get-tuple-element.60), channel_id=1, source_target_pairs={{0,64},{4,20},{8,72},{12,28},{16,80},{20,4},{24,88},{28,12},{32,96... | collective-permute-start | bytes 1179656 | tf_op jit(solution)/shard_map/ppermute | solution.py:329
  68.7 0.5 collective-permute-start.22
  69.2 0.0 collective-permute-start.12
  69.2 8.4 %collective-permute-done.21.refs_9_ = f32[4,192,128]{2,1,0:T(8,128)S(1)} collective-permute-done((f32[4,192,128]{2,1,0:T(8,128)S(1)}, f32[4,192,128]{2,1,0:T(8,128)S(1)}, u32[]{:S(2)}, u32[]{:S(2)}) %collective-permute-start.21) | collective-permute-done | bytes 393248 | tf_op jit(solution)/shard_map/ppermute | solution.py:329
  77.6 0.0 collective-permute-start.13
  77.6 4.1 %collective-permute-done.22.refs_10_ = f32[4,192,128]{2,1,0:T(8,128)S(1)} collective-permute-done((f32[4,192,128]{2,1,0:T(8,128)S(1)}, f32[4,192,128]{2,1,0:T(8,128)S(1)}, u32[]{:S(2)}, u32[]{:S(2)}) %collective-permute-start.22) | collective-permute-done | bytes 393248 | tf_op jit(solution)/shard_map/ppermute | solution.py:329
  81.7 1.2 %collective-permute-start.7 = (f32[4,200,128]{2,1,0:T(8,128)S(1)}, f32[4,200,128]{2,1,0:T(8,128)S(1)}, u32[]{:S(2)}, u32[]{:S(2)}) collective-permute-start(f32[4,200,128]{2,1,0:T(8,128)S(1)} %get-tuple-element.44), channel_id=1, source_target_pairs={{0,64},{4,20},{8,72},{12,28},{16,80},{20,4},{24,88},{28,12},{32,96... | collective-permute-start | bytes 1228808 | tf_op jit(solution)/shard_map/ppermute | solution.py:329
  82.9 0.0 collective-permute-done.10.refs_4_
  82.9 0.2 collective-permute-start.8
  83.1 0.0 collective-permute-done.11.refs_5_
  83.1 3.0 %collective-permute-start.9 = (f32[4,200,128]{2,1,0:T(8,128)S(1)}, f32[4,200,128]{2,1,0:T(8,128)S(1)}, u32[]{:S(2)}, u32[]{:S(2)}) collective-permute-start(f32[4,200,128]{2,1,0:T(8,128)S(1)} %get-tuple-element.46), channel_id=1, source_target_pairs={{0,96},{4,28},{8,104},{12,4},{16,112},{20,12},{24,120},{28,20},{32... | collective-permute-start | bytes 1228808 | tf_op jit(solution)/shard_map/ppermute | solution.py:329
  86.1 0.1 collective-permute-start.23
  86.2 0.0 collective-permute-done.13.refs_7_
  86.2 2.9 %collective-permute-start.24 = (f32[4,192,128]{2,1,0:T(8,128)S(1)}, f32[4,192,128]{2,1,0:T(8,128)S(1)}, u32[]{:S(2)}, u32[]{:S(2)}) collective-permute-start(f32[4,192,128]{2,1,0:T(8,128)S(1)} %get-tuple-element.63), channel_id=1, source_target_pairs={{0,68},{4,16},{8,76},{12,24},{16,84},{20,0},{24,92},{28,8},{32,100... | collective-permute-start | bytes 1179656 | tf_op jit(solution)/shard_map/ppermute | solution.py:329
  89.1 2.1 %collective-permute-done.7.refs_1_ = f32[4,200,128]{2,1,0:T(8,128)S(1)} collective-permute-done((f32[4,200,128]{2,1,0:T(8,128)S(1)}, f32[4,200,128]{2,1,0:T(8,128)S(1)}, u32[]{:S(2)}, u32[]{:S(2)}) %collective-permute-start.7) | collective-permute-done | bytes 409632 | tf_op jit(solution)/shard_map/ppermute | solution.py:329
  91.2 4.3 %collective-permute-done.8.refs_2_ = f32[4,200,128]{2,1,0:T(8,128)S(1)} collective-permute-done((f32[4,200,128]{2,1,0:T(8,128)S(1)}, f32[4,200,128]{2,1,0:T(8,128)S(1)}, u32[]{:S(2)}, u32[]{:S(2)}) %collective-permute-start.8) | collective-permute-done | bytes 409632 | tf_op jit(solution)/shard_map/ppermute | solution.py:329
  95.5 1.4 %collective-permute-start.26 = (f32[4,192,128]{2,1,0:T(8,128)S(1)}, f32[4,192,128]{2,1,0:T(8,128)S(1)}, u32[]{:S(2)}, u32[]{:S(2)}) collective-permute-start(f32[4,192,128]{2,1,0:T(8,128)S(1)} %get-tuple-element.65), channel_id=1, source_target_pairs={{0,100},{4,24},{8,108},{12,0},{16,116},{20,8},{24,124},{28,16},{32... | collective-permute-start | bytes 1179656 | tf_op jit(solution)/shard_map/ppermute | solution.py:329
  96.9 0.0 collective-permute-done.9.refs_3_
  96.9 1.7 %collective-permute-start.27 = (f32[4,192,128]{2,1,0:T(8,128)S(1)}, f32[4,192,128]{2,1,0:T(8,128)S(1)}, u32[]{:S(2)}, u32[]{:S(2)}) collective-permute-start(f32[4,192,128]{2,1,0:T(8,128)S(1)} %get-tuple-element.66), channel_id=1, source_target_pairs={{0,4},{4,0},{8,12},{12,8},{16,20},{20,16},{24,28},{28,24},{32,36},... | collective-permute-start | bytes 1179656 | tf_op jit(solution)/shard_map/ppermute | solution.py:329
  98.7 5.0 %couple.1 = f32[3,256,384]{2,1,0:T(8,128)} custom-call(f32[3,3072]{1,0:T(4,128)S(1)} %copy-done, bf16[3,3072,384]{2,1,0:T(8,128)(2,1)S(1)} %bitcast.1, bf16[3,3072,256]{2,1,0:T(8,128)(2,1)S(1)} %bitcast.3), custom_call_target="tpu_custom_call" | custom-call | flops 1811939328 | bytes 12000000 | tf_op jit(solution)/shard_map/couple/pallas_call | solution.py:127
  103.7 2.5 %assemble.2 = f32[24,4,32,128]{3,2,1,0:T(8,128)} custom-call(f32[4,200,128]{2,1,0:T(8,128)S(1)} %get-tuple-element.43.refs_0_, f32[4,200,128]{2,1,0:T(8,128)S(1)} %collective-permute-done.7.refs_1_, f32[4,200,128]{2,1,0:T(8,128)S(1)} %collective-permute-done.8.refs_2_, f32[4,200,128]{2,1,0:T(8,128)S(1)} %collective-permute-done.9.refs_3_, ...), custom_call_target="tpu_custom_call" | custom-call | flops 4000000 | bytes 6000000 | tf_op jit(solution)/shard_map/assemble/pallas_call | solution.py:284
  106.2 0.0 collective-permute-done.24.refs_12_
  106.2 0.0 collective-permute-done.25.refs_13_
  106.2 0.0 collective-permute-done.27.refs_15_
  106.2 2.5 %assemble.3 = f32[24,4,32,128]{3,2,1,0:T(8,128)} custom-call(f32[4,200,128]{2,1,0:T(8,128)S(1)} %get-tuple-element.43.refs_0_, f32[4,200,128]{2,1,0:T(8,128)S(1)} %collective-permute-done.7.refs_1_, f32[4,200,128]{2,1,0:T(8,128)S(1)} %collective-permute-done.8.refs_2_, f32[4,200,128]{2,1,0:T(8,128)S(1)} %collective-permute-done.9.refs_3_, ...), custom_call_target="tpu_custom_call" | custom-call | flops 4000000 | bytes 6000000 | tf_op jit(solution)/shard_map/assemble/pallas_call | solution.py:284
  (15 shorter events, 0.0 us)
Async XLA Ops:
  0.6 14.4 %copy-start = (f32[3,3072]{1,0:T(4,128)S(1)}, f32[3,3072]{1,0:T(4,128)}, u32[]{:S(2)}) copy-start(f32[3,3072]{1,0:T(4,128)} %im.3) | copy-start | bytes 110596
  7.8 15.6 %collective-permute-start = (f32[3,200,128]{2,1,0:T(8,128)S(1)}, f32[3,200,128]{2,1,0:T(8,128)S(1)}, u32[]{:S(2)}, u32[]{:S(2)}) collective-permute-start(f32[3,200,128]{2,1,0:T(8,128)S(1)} %get-tuple-element.36), channel_id=1, source_target_pairs={{0,2},{1,3},{2,0},{3,1},{4,6},{5,7},{6,4},{7,5},{8,10},{9,11},{10,... | collective-permute-start | bytes 921608 | tf_op jit(solution)/shard_map/ppermute | solution.py:319
  11.8 14.2 %collective-permute-start.1 = (f32[3,200,128]{2,1,0:T(8,128)S(1)}, f32[3,200,128]{2,1,0:T(8,128)S(1)}, u32[]{:S(2)}, u32[]{:S(2)}) collective-permute-start(f32[3,200,128]{2,1,0:T(8,128)S(1)} %get-tuple-element.37), channel_id=1, source_target_pairs={{0,1},{1,2},{2,3},{3,0},{4,5},{5,6},{6,7},{7,4},{8,9},{9,10},{10,1... | collective-permute-start | bytes 921608 | tf_op jit(solution)/shard_map/ppermute | solution.py:319
  12.8 14.7 %collective-permute-start.2 = (f32[3,200,128]{2,1,0:T(8,128)S(1)}, f32[3,200,128]{2,1,0:T(8,128)S(1)}, u32[]{:S(2)}, u32[]{:S(2)}) collective-permute-start(f32[3,200,128]{2,1,0:T(8,128)S(1)} %get-tuple-element.38), channel_id=1, source_target_pairs={{0,3},{1,0},{2,1},{3,2},{4,7},{5,4},{6,5},{7,6},{8,11},{9,8},{10,9... | collective-permute-start | bytes 921608 | tf_op jit(solution)/shard_map/ppermute | solution.py:319
  22.4 11.5 %collective-permute-start.14 = (f32[3,192,128]{2,1,0:T(8,128)S(1)}, f32[3,192,128]{2,1,0:T(8,128)S(1)}, u32[]{:S(2)}, u32[]{:S(2)}) collective-permute-start(f32[3,192,128]{2,1,0:T(8,128)S(1)} %get-tuple-element.52), channel_id=1, source_target_pairs={{0,2},{1,3},{2,0},{3,1},{4,6},{5,7},{6,4},{7,5},{8,10},{9,11},{10,... | collective-permute-start | bytes 884744 | tf_op jit(solution)/shard_map/ppermute | solution.py:319
  22.5 15.8 %collective-permute-start.15 = (f32[3,192,128]{2,1,0:T(8,128)S(1)}, f32[3,192,128]{2,1,0:T(8,128)S(1)}, u32[]{:S(2)}, u32[]{:S(2)}) collective-permute-start(f32[3,192,128]{2,1,0:T(8,128)S(1)} %get-tuple-element.53), channel_id=1, source_target_pairs={{0,1},{1,2},{2,3},{3,0},{4,5},{5,6},{6,7},{7,4},{8,9},{9,10},{10,1... | collective-permute-start | bytes 884744 | tf_op jit(solution)/shard_map/ppermute | solution.py:319
  23.4 15.8 %collective-permute-start.16 = (f32[3,192,128]{2,1,0:T(8,128)S(1)}, f32[3,192,128]{2,1,0:T(8,128)S(1)}, u32[]{:S(2)}, u32[]{:S(2)}) collective-permute-start(f32[3,192,128]{2,1,0:T(8,128)S(1)} %get-tuple-element.54), channel_id=1, source_target_pairs={{0,3},{1,0},{2,1},{3,2},{4,7},{5,4},{6,5},{7,6},{8,11},{9,8},{10,9... | collective-permute-start | bytes 884744 | tf_op jit(solution)/shard_map/ppermute | solution.py:319
  28.2 14.9 %collective-permute-start.3 = (f32[8,200,128]{2,1,0:T(8,128)S(1)}, f32[8,200,128]{2,1,0:T(8,128)S(1)}, u32[]{:S(2)}, u32[]{:S(2)}) collective-permute-start(f32[8,200,128]{2,1,0:T(8,128)S(1)} %get-tuple-element.39), channel_id=1, source_target_pairs={{0,8},{4,36},{8,16},{12,44},{16,24},{20,52},{24,0},{28,60},{32,40}... | collective-permute-start | bytes 2457608 | tf_op jit(solution)/shard_map/ppermute | solution.py:324
  29.7 13.3 %collective-permute-start.4 = (f32[8,200,128]{2,1,0:T(8,128)S(1)}, f32[8,200,128]{2,1,0:T(8,128)S(1)}, u32[]{:S(2)}, u32[]{:S(2)}) collective-permute-start(f32[8,200,128]{2,1,0:T(8,128)S(1)} %get-tuple-element.40), channel_id=1, source_target_pairs={{0,24},{4,100},{8,0},{12,108},{16,8},{20,116},{24,16},{28,124},{32... | collective-permute-start | bytes 2457608 | tf_op jit(solution)/shard_map/ppermute | solution.py:324
  39.7 13.3 %collective-permute-start.17 = (f32[8,192,128]{2,1,0:T(8,128)S(1)}, f32[8,192,128]{2,1,0:T(8,128)S(1)}, u32[]{:S(2)}, u32[]{:S(2)}) collective-permute-start(f32[8,192,128]{2,1,0:T(8,128)S(1)} %get-tuple-element.55), channel_id=1, source_target_pairs={{0,8},{4,36},{8,16},{12,44},{16,24},{20,52},{24,0},{28,60},{32,40}... | collective-permute-start | bytes 2359304 | tf_op jit(solution)/shard_map/ppermute | solution.py:324
  41.3 12.0 %collective-permute-start.18 = (f32[8,192,128]{2,1,0:T(8,128)S(1)}, f32[8,192,128]{2,1,0:T(8,128)S(1)}, u32[]{:S(2)}, u32[]{:S(2)}) collective-permute-start(f32[8,192,128]{2,1,0:T(8,128)S(1)} %get-tuple-element.56), channel_id=1, source_target_pairs={{0,24},{4,100},{8,0},{12,108},{16,8},{20,116},{24,16},{28,124},{32... | collective-permute-start | bytes 2359304 | tf_op jit(solution)/shard_map/ppermute | solution.py:324
  43.0 55.6 %slice-start = ((s8[7077888]{0:T(1024)(128)(4,1)}), s8[4194304]{0:T(1024)(128)(4,1)S(1)}, s32[]{:S(2)}) async-start(s8[7077888]{0:T(1024)(128)(4,1)} %bitcast), calls=%async_computation | async-start | bytes 8388608
  43.0 55.6 %slice-start.2 = ((s8[4718592]{0:T(1024)(128)(4,1)}), s8[4194304]{0:T(1024)(128)(4,1)S(1)}, s32[]{:S(2)}) async-start(s8[4718592]{0:T(1024)(128)(4,1)} %bitcast.2), calls=%async_computation.2 | async-start | bytes 8388608
  43.8 13.6 %collective-permute-start.5 = (f32[4,200,128]{2,1,0:T(8,128)S(1)}, f32[4,200,128]{2,1,0:T(8,128)S(1)}, u32[]{:S(2)}, u32[]{:S(2)}) collective-permute-start(f32[4,200,128]{2,1,0:T(8,128)S(1)} %get-tuple-element.41), channel_id=1, source_target_pairs={{0,8},{4,36},{8,16},{12,44},{16,24},{20,52},{24,0},{28,60},{32,40}... | collective-permute-start | bytes 1228808 | tf_op jit(solution)/shard_map/ppermute | solution.py:324
  44.4 13.3 %collective-permute-start.6 = (f32[4,200,128]{2,1,0:T(8,128)S(1)}, f32[4,200,128]{2,1,0:T(8,128)S(1)}, u32[]{:S(2)}, u32[]{:S(2)}) collective-permute-start(f32[4,200,128]{2,1,0:T(8,128)S(1)} %get-tuple-element.42), channel_id=1, source_target_pairs={{0,24},{4,100},{8,0},{12,108},{16,8},{20,116},{24,16},{28,124},{32... | collective-permute-start | bytes 1228808 | tf_op jit(solution)/shard_map/ppermute | solution.py:324
  54.0 9.9 %collective-permute-start.19 = (f32[4,192,128]{2,1,0:T(8,128)S(1)}, f32[4,192,128]{2,1,0:T(8,128)S(1)}, u32[]{:S(2)}, u32[]{:S(2)}) collective-permute-start(f32[4,192,128]{2,1,0:T(8,128)S(1)} %get-tuple-element.57), channel_id=1, source_target_pairs={{0,8},{4,36},{8,16},{12,44},{16,24},{20,52},{24,0},{28,60},{32,40}... | collective-permute-start | bytes 1179656 | tf_op jit(solution)/shard_map/ppermute | solution.py:324
  55.6 43.1 %slice-start.1 = ((s8[7077888]{0:T(1024)(128)(4,1)}), s8[2883584]{0:T(1024)(128)(4,1)S(1)}, s32[]{:S(2)}) async-start(s8[7077888]{0:T(1024)(128)(4,1)} %bitcast), calls=%async_computation.1 | async-start | bytes 5767168
  55.6 43.1 %slice-start.3 = ((s8[4718592]{0:T(1024)(128)(4,1)}), s8[524288]{0:T(1024)(128)(4,1)S(1)}, s32[]{:S(2)}) async-start(s8[4718592]{0:T(1024)(128)(4,1)} %bitcast.2), calls=%async_computation.3 | async-start | bytes 1048576
  55.6 8.4 %collective-permute-start.20 = (f32[4,192,128]{2,1,0:T(8,128)S(1)}, f32[4,192,128]{2,1,0:T(8,128)S(1)}, u32[]{:S(2)}, u32[]{:S(2)}) collective-permute-start(f32[4,192,128]{2,1,0:T(8,128)S(1)} %get-tuple-element.58), channel_id=1, source_target_pairs={{0,24},{4,100},{8,0},{12,108},{16,8},{20,116},{24,16},{28,124},{32... | collective-permute-start | bytes 1179656 | tf_op jit(solution)/shard_map/ppermute | solution.py:324
  59.6 23.3 %collective-permute-start.10 = (f32[4,200,128]{2,1,0:T(8,128)S(1)}, f32[4,200,128]{2,1,0:T(8,128)S(1)}, u32[]{:S(2)}, u32[]{:S(2)}) collective-permute-start(f32[4,200,128]{2,1,0:T(8,128)S(1)} %get-tuple-element.47), channel_id=1, source_target_pairs={{0,68},{4,16},{8,76},{12,24},{16,84},{20,0},{24,92},{28,8},{32,100... | collective-permute-start | bytes 1228808 | tf_op jit(solution)/shard_map/ppermute | solution.py:329
  60.6 22.5 %collective-permute-start.11 = (f32[4,200,128]{2,1,0:T(8,128)S(1)}, f32[4,200,128]{2,1,0:T(8,128)S(1)}, u32[]{:S(2)}, u32[]{:S(2)}) collective-permute-start(f32[4,200,128]{2,1,0:T(8,128)S(1)} %get-tuple-element.48), channel_id=1, source_target_pairs={{0,36},{4,8},{8,44},{12,16},{16,52},{20,24},{24,60},{28,0},{32,68}... | collective-permute-start | bytes 1228808 | tf_op jit(solution)/shard_map/ppermute | solution.py:329
  65.7 11.8 %collective-permute-start.21 = (f32[4,192,128]{2,1,0:T(8,128)S(1)}, f32[4,192,128]{2,1,0:T(8,128)S(1)}, u32[]{:S(2)}, u32[]{:S(2)}) collective-permute-start(f32[4,192,128]{2,1,0:T(8,128)S(1)} %get-tuple-element.60), channel_id=1, source_target_pairs={{0,64},{4,20},{8,72},{12,28},{16,80},{20,4},{24,88},{28,12},{32,96... | collective-permute-start | bytes 1179656 | tf_op jit(solution)/shard_map/ppermute | solution.py:329
  68.7 13.0 %collective-permute-start.22 = (f32[4,192,128]{2,1,0:T(8,128)S(1)}, f32[4,192,128]{2,1,0:T(8,128)S(1)}, u32[]{:S(2)}, u32[]{:S(2)}) collective-permute-start(f32[4,192,128]{2,1,0:T(8,128)S(1)} %get-tuple-element.61), channel_id=1, source_target_pairs={{0,32},{4,12},{8,40},{12,20},{16,48},{20,28},{24,56},{28,4},{32,64... | collective-permute-start | bytes 1179656 | tf_op jit(solution)/shard_map/ppermute | solution.py:329
  69.2 17.0 %collective-permute-start.12 = (f32[4,200,128]{2,1,0:T(8,128)S(1)}, f32[4,200,128]{2,1,0:T(8,128)S(1)}, u32[]{:S(2)}, u32[]{:S(2)}) collective-permute-start(f32[4,200,128]{2,1,0:T(8,128)S(1)} %get-tuple-element.49), channel_id=1, source_target_pairs={{0,100},{4,24},{8,108},{12,0},{16,116},{20,8},{24,124},{28,16},{32... | collective-permute-start | bytes 1228808 | tf_op jit(solution)/shard_map/ppermute | solution.py:329
  77.6 8.7 %collective-permute-start.13 = (f32[4,200,128]{2,1,0:T(8,128)S(1)}, f32[4,200,128]{2,1,0:T(8,128)S(1)}, u32[]{:S(2)}, u32[]{:S(2)}) collective-permute-start(f32[4,200,128]{2,1,0:T(8,128)S(1)} %get-tuple-element.50), channel_id=1, source_target_pairs={{0,4},{4,0},{8,12},{12,8},{16,20},{20,16},{24,28},{28,24},{32,36},... | collective-permute-start | bytes 1228808 | tf_op jit(solution)/shard_map/ppermute | solution.py:329
  81.7 9.6 %collective-permute-start.7 = (f32[4,200,128]{2,1,0:T(8,128)S(1)}, f32[4,200,128]{2,1,0:T(8,128)S(1)}, u32[]{:S(2)}, u32[]{:S(2)}) collective-permute-start(f32[4,200,128]{2,1,0:T(8,128)S(1)} %get-tuple-element.44), channel_id=1, source_target_pairs={{0,64},{4,20},{8,72},{12,28},{16,80},{20,4},{24,88},{28,12},{32,96... | collective-permute-start | bytes 1228808 | tf_op jit(solution)/shard_map/ppermute | solution.py:329
  82.9 12.6 %collective-permute-start.8 = (f32[4,200,128]{2,1,0:T(8,128)S(1)}, f32[4,200,128]{2,1,0:T(8,128)S(1)}, u32[]{:S(2)}, u32[]{:S(2)}) collective-permute-start(f32[4,200,128]{2,1,0:T(8,128)S(1)} %get-tuple-element.45), channel_id=1, source_target_pairs={{0,32},{4,12},{8,40},{12,20},{16,48},{20,28},{24,56},{28,4},{32,64... | collective-permute-start | bytes 1228808 | tf_op jit(solution)/shard_map/ppermute | solution.py:329
  83.1 13.8 %collective-permute-start.9 = (f32[4,200,128]{2,1,0:T(8,128)S(1)}, f32[4,200,128]{2,1,0:T(8,128)S(1)}, u32[]{:S(2)}, u32[]{:S(2)}) collective-permute-start(f32[4,200,128]{2,1,0:T(8,128)S(1)} %get-tuple-element.46), channel_id=1, source_target_pairs={{0,96},{4,28},{8,104},{12,4},{16,112},{20,12},{24,120},{28,20},{32... | collective-permute-start | bytes 1228808 | tf_op jit(solution)/shard_map/ppermute | solution.py:329
  86.1 20.0 %collective-permute-start.23 = (f32[4,192,128]{2,1,0:T(8,128)S(1)}, f32[4,192,128]{2,1,0:T(8,128)S(1)}, u32[]{:S(2)}, u32[]{:S(2)}) collective-permute-start(f32[4,192,128]{2,1,0:T(8,128)S(1)} %get-tuple-element.62), channel_id=1, source_target_pairs={{0,96},{4,28},{8,104},{12,4},{16,112},{20,12},{24,120},{28,20},{32... | collective-permute-start | bytes 1179656 | tf_op jit(solution)/shard_map/ppermute | solution.py:329
  86.2 19.9 %collective-permute-start.24 = (f32[4,192,128]{2,1,0:T(8,128)S(1)}, f32[4,192,128]{2,1,0:T(8,128)S(1)}, u32[]{:S(2)}, u32[]{:S(2)}) collective-permute-start(f32[4,192,128]{2,1,0:T(8,128)S(1)} %get-tuple-element.63), channel_id=1, source_target_pairs={{0,68},{4,16},{8,76},{12,24},{16,84},{20,0},{24,92},{28,8},{32,100... | collective-permute-start | bytes 1179656 | tf_op jit(solution)/shard_map/ppermute | solution.py:329
  91.2 14.9 %collective-permute-start.25 = (f32[4,192,128]{2,1,0:T(8,128)S(1)}, f32[4,192,128]{2,1,0:T(8,128)S(1)}, u32[]{:S(2)}, u32[]{:S(2)}) collective-permute-start(f32[4,192,128]{2,1,0:T(8,128)S(1)} %get-tuple-element.64), channel_id=1, source_target_pairs={{0,36},{4,8},{8,44},{12,16},{16,52},{20,24},{24,60},{28,0},{32,68}... | collective-permute-start | bytes 1179656 | tf_op jit(solution)/shard_map/ppermute | solution.py:329
  95.5 10.7 %collective-permute-start.26 = (f32[4,192,128]{2,1,0:T(8,128)S(1)}, f32[4,192,128]{2,1,0:T(8,128)S(1)}, u32[]{:S(2)}, u32[]{:S(2)}) collective-permute-start(f32[4,192,128]{2,1,0:T(8,128)S(1)} %get-tuple-element.65), channel_id=1, source_target_pairs={{0,100},{4,24},{8,108},{12,0},{16,116},{20,8},{24,124},{28,16},{32... | collective-permute-start | bytes 1179656 | tf_op jit(solution)/shard_map/ppermute | solution.py:329
  96.9 9.3 %collective-permute-start.27 = (f32[4,192,128]{2,1,0:T(8,128)S(1)}, f32[4,192,128]{2,1,0:T(8,128)S(1)}, u32[]{:S(2)}, u32[]{:S(2)}) collective-permute-start(f32[4,192,128]{2,1,0:T(8,128)S(1)} %get-tuple-element.66), channel_id=1, source_target_pairs={{0,4},{4,0},{8,12},{12,8},{16,20},{20,16},{24,28},{28,24},{32,36},... | collective-permute-start | bytes 1179656 | tf_op jit(solution)/shard_map/ppermute | solution.py:329
